TPU v7x, 128 devices: a whole 4x4x4 slice. The times are simulated.
128 devices in a mesh: group: 2 (over z_hi), slab: 64 (over y, x, z_lo, core).
Axes of the slice: x: 4, y: 4, z: 4 (z_hi: 2, z_lo: 2; z = z_hi * 2 + z_lo), core: 2. Of those that a mesh axis runs over, the one named last changes fastest.
Arguments:
- queries: bfloat16 [65536, 512], P(('group', 'slab')), may hold values from -6 to 6
- keys: bfloat16 [65536, 512], P(('group', 'slab')), may hold values from -6 to 6
- values: bfloat16 [65536, 512], P(('group', 'slab')), may hold values from -6 to 6
- neighbours: int32 [512, 6], P(('group', 'slab')), may hold values from 0 to 15, as said below
- live_tiles: int32 [128], P(('group', 'slab')), may hold values from 1 to 4, as said below
- boundary_ids: int32 [128, 4], P(('group', 'slab')), may hold values from 0 to 3, as said below
Outputs:
- attended: bfloat16 [65536, 512], P(('group', 'slab'))
Inputs may be any that keep to these rules, and one draw needn't show every extreme that they name: `neighbours`: each row names 6 different positions of the pool. `live_tiles`: some slab has all 4 tiles active. `boundary_ids`: each row names 4 different tiles of its slab.
All inputs are finite; a program needn't handle non-finite values.
Results may differ from a plain program's by a relative error of at most 0.008.
Values may be sent and summed in bfloat16 or wider, within the bound.
No kernel may reach another device: no remote copies, remote signals or barrier semaphores. Data moves between devices by JAX's collectives and lax.ppermute only.
A program may use at most 128 MiB of HBM per device.

v0:
```python
import jax
import jax.numpy as jnp
from jax import lax
from jax.sharding import PartitionSpec as P

HEADS = 8
HEAD_DIM = 64
TILE = 128
HALO = 4
BLOCK = 4


def shifted(block, axis, distance):
    devices = range(lax.axis_size(axis))
    route = [((i - distance) % len(devices), i) for i in devices]
    return lax.ppermute(block, axis, route)


def attend_block(number, tile_queries, pool, lists, live):
    width = tile_queries.shape[2]
    tile = tile_queries.shape[1]
    start = number * BLOCK
    listed = lists.shape[1]
    key_set = pool[0][lists].reshape(BLOCK, listed * tile, HEADS, HEAD_DIM)
    value_set = pool[1][lists].reshape(BLOCK, listed * tile, HEADS, HEAD_DIM)
    query_set = tile_queries.reshape(BLOCK, tile, HEADS, HEAD_DIM)
    scores = jnp.einsum(
        "qihd,qjhd->qhij", query_set, key_set, preferred_element_type=jnp.float32
    ) * HEAD_DIM ** (-0.5)
    weights = jax.nn.softmax(scores, axis=-1).astype(jnp.bfloat16)
    mixed = jnp.einsum("qhij,qjhd->qihd", weights, value_set, preferred_element_type=jnp.float32)
    alive = start + jnp.arange(BLOCK, dtype=jnp.int32) < live
    mixed = jnp.where(alive[:, None, None, None], mixed, 0.0)
    return mixed.astype(jnp.bfloat16).reshape(BLOCK, tile, width)


def shards(queries, keys, values, neighbours, live_tiles, boundary_ids):
    tile = TILE
    count = queries.shape[0] // tile
    width = queries.shape[1]
    pairs = jnp.stack([keys, values])
    before = shifted(pairs, "slab", 1)
    after = shifted(pairs, "slab", -1)
    tiled = pairs.reshape(2, count, tile, width)
    remote, remote_ids = shifted((tiled, boundary_ids), "group", 1)
    border = remote[:, remote_ids[0]]
    pool = jnp.concatenate(
        [tiled, before.reshape(2, HALO, tile, width), after.reshape(2, HALO, tile, width), border],
        axis=1,
    )
    tile_queries = queries.reshape(count, tile, width)
    live = live_tiles[0]
    blocks = count // BLOCK
    outputs = lax.map(
        lambda number: attend_block(number, tile_queries, pool, neighbours, live),
        jnp.arange(blocks, dtype=jnp.int32),
    )
    result = outputs.reshape(count * tile, width)
    return result


def solution(mesh):
    in_specs = (
        P(("group", "slab"), None),
        P(("group", "slab"), None),
        P(("group", "slab"), None),
        P(("group", "slab"), None),
        P(("group", "slab")),
        P(("group", "slab"), None),
    )
    out_specs = P(("group", "slab"), None)
    return jax.shard_map(shards, mesh=mesh, in_specs=in_specs, out_specs=out_specs, check_vma=False)
```

profile of v0, /device:TPU:1, one launch (start us, length us, event | category | flops | bytes accessed | tf_op | source)
XLA Modules:
  0.0 120.8 jit_solution(13896946493325946148)
XLA Ops:
  0.0 0.0 copy-start.1
  0.0 0.0 copy-start
  0.0 1.4 %pad_maximum_fusion.1 = bf16[2,4,128,512]{3,2,0,1:T(8,128)(2,1)S(1)} fusion(bf16[1,4,128,512]{3,2,0,1:T(8,128)(2,1)} %bitcast.40, bf16[1,4,128,512]{3,2,0,1:T(8,128)(2,1)} %bitcast.43), kind=kLoop, calls=%fused_computation.21 | loop fusion | flops 524288 | bytes 2097152 | tf_op jit(solution)/shard_map/stack | solution.py:41
  1.4 4.5 %collective-permute-start.2 = (bf16[2,4,128,512]{3,2,0,1:T(8,128)(2,1)S(1)}, bf16[2,4,128,512]{3,2,0,1:T(8,128)(2,1)}, u32[]{:S(2)}, u32[]{:S(2)}) collective-permute-start(bf16[2,4,128,512]{3,2,0,1:T(8,128)(2,1)S(1)} %pad_maximum_fusion.1), channel_id=1, source_target_pairs={{64,0},{0,64},{65,1},{1,65},{66,2},{2,66},{67,3},{3,67},{68,4},{4,... | collective-permute-start | bytes 3145736 | tf_op jit(solution)/shard_map/ppermute | solution.py:16
  5.9 2.3 %pad_maximum_fusion.2 = bf16[2,512,512]{2,1,0:T(8,128)(2,1)} fusion(bf16[1,512,512]{2,1,0:T(8,128)(2,1)} %bitcast.41, bf16[1,512,512]{2,1,0:T(8,128)(2,1)} %bitcast.44), kind=kLoop, calls=%fused_computation.22 | loop fusion | flops 524288 | bytes 2097152 | tf_op jit(solution)/shard_map/stack | solution.py:41
  8.2 1.6 %collective-permute-start = (bf16[2,512,512]{2,1,0:T(8,128)(2,1)}, bf16[2,512,512]{2,1,0:T(8,128)(2,1)}, u32[]{:S(2)}, u32[]{:S(2)}) collective-permute-start(bf16[2,512,512]{2,1,0:T(8,128)(2,1)} %pad_maximum_fusion.2), channel_id=1, source_target_pairs={{63,0},{0,1},{1,2},{2,3},{3,4},{4,5},{5,6},{6,7},{7,8},{8,9},{9,10... | collective-permute-start | bytes 3145736 | tf_op jit(solution)/shard_map/ppermute | solution.py:16
  9.8 0.0 collective-permute-start.1
  9.8 0.9 collective-permute-start.3
  10.6 0.7 compare_select_fusion
  11.3 0.1 reshape.75
  11.4 1.6 %reshape.97 = bf16[4,128,8,64]{3,2,1,0:T(8,128)(2,1)S(1)} reshape(bf16[512,512]{1,0:T(8,128)(2,1)} %param.6) | data formatting | bytes 1048576 | tf_op jit(solution)/shard_map/while/body/eval_jaxpr/reshape;reshape | solution.py:26
  13.7 38.1 %collective-permute-done.3 = s32[1,4]{1,0:T(1,128)S(1)} collective-permute-done((s32[1,4]{1,0:T(1,128)}, s32[1,4]{1,0:T(1,128)S(1)}, u32[]{:S(2)}, u32[]{:S(2)}) %collective-permute-start.3) | collective-permute-done | bytes 48 | tf_op jit(solution)/shard_map/ppermute | solution.py:16
  51.8 0.0 collective-permute-done.2
  51.8 1.3 %copy.19 = bf16[2,4,128,512]{3,2,1,0:T(8,128)(2,1)S(1)} copy(bf16[2,4,128,512]{3,2,0,1:T(8,128)(2,1)} %collective-permute-done.2) | data formatting | bytes 2097152 | tf_op jit(solution)/shard_map/ppermute | solution.py:16
  53.2 1.6 %gather_fusion = bf16[4,2,128,512]{3,2,1,0:T(8,128)(2,1)} fusion(bf16[2,4,128,512]{3,2,1,0:T(8,128)(2,1)S(1)} %copy.19, s32[1024]{0:T(1024)S(1)} %pad_clamp_fusion.1), kind=kCustom, calls=%fused_computation | custom fusion | bytes 2097168 | tf_op jit(solution)/shard_map/gather | solution.py:46
  54.7 0.0 collective-permute-done
  54.8 0.0 collective-permute-done.1
  54.8 0.0 copy-done.1
  54.8 0.0 copy-done
  54.8 2.0 %pad_maximum_fusion = bf16[2,16,128,512]{3,2,0,1:T(8,128)(2,1)S(1)} fusion(bf16[2,4,128,512]{3,2,0,1:T(8,128)(2,1)} %bitcast.46, bf16[1,4,128,512]{3,2,0,1:T(8,128)(2,1)S(1)} %bitcast.42, bf16[1,4,128,512]{3,2,0,1:T(8,128)(2,1)S(1)} %bitcast.45, bf16[2,4,128,512]{3,2,1,0:T(8,128)(2,1)} %bitcast.5, bf16[2,4,128,512]{3,2,1,0:T(8,128)(2,1)} %bitcast.6), kind=kLoop, calls=%fused_computation.15 | loop fusion | flops 20971520 | bytes 8388608 | tf_op jit(solution)/shard_map/concatenate | solution.py:47
  56.8 1.6 %slice_bitcast_fusion.1 = (bf16[16,128,512]{2,1,0:T(8,128)(2,1)S(1)}, bf16[16,128,512]{2,1,0:T(8,128)(2,1)}) fusion(bf16[2,16,128,512]{3,2,0,1:T(8,128)(2,1)S(1)} %pad_maximum_fusion), kind=kLoop, calls=%fused_computation.17 | loop fusion | bytes 8388608 | tf_op jit(solution)/shard_map/while/body/eval_jaxpr/squeeze | solution.py:25
  58.5 4.1 %gather_fusion.2 = bf16[24,128,512]{2,1,0:T(8,128)(2,1)} fusion(bf16[16,128,512]{2,1,0:T(8,128)(2,1)} %get-tuple-element.16, s32[1024]{0:T(1024)S(1)} %pad_clamp_fusion), kind=kCustom, calls=%fused_computation.2 | custom fusion | bytes 6291552 | tf_op jit(solution)/shard_map/while/body/eval_jaxpr/gather | solution.py:24
  62.6 8.9 %reshape.96 = bf16[4,768,8,64]{3,2,1,0:T(8,128)(2,1)} reshape(bf16[24,128,512]{2,1,0:T(8,128)(2,1)} %gather_fusion.2) | data formatting | bytes 6291456 | tf_op jit(solution)/shard_map/while/body/eval_jaxpr/reshape | solution.py:24
  71.5 9.2 %fusion.6 = f32[4,8,768,128]{3,2,1,0:T(8,128)} fusion(bf16[4,768,8,64]{3,2,1,0:T(8,128)(2,1)} %reshape.96, bf16[4,128,8,64]{3,2,1,0:T(8,128)(2,1)S(1)} %reshape.97), kind=kOutput, calls=%fused_computation.10 | convolution fusion | flops 402653184 | bytes 16252928 | tf_op jit(solution)/shard_map/while/body/eval_jaxpr/qihd,qjhd->qhij/dot_general | solution.py:27
  80.6 11.1 %fusion.30 = f32[4,8,128]{2,1,0:T(8,128)S(1)} fusion(f32[4,8,768,128]{3,2,1,0:T(8,128)} %fusion.6), kind=kOutput, calls=%fused_computation.33 | output fusion | flops 12583679 | bytes 12599296 | tf_op jit(solution)/shard_map/while/body/eval_jaxpr/sub | solution.py:30
  91.8 2.5 %gather_fusion.1 = bf16[24,128,512]{2,1,0:T(8,128)(2,1)} fusion(bf16[16,128,512]{2,1,0:T(8,128)(2,1)S(1)} %get-tuple-element.15, s32[1024]{0:T(1024)S(1)} %pad_clamp_fusion), kind=kCustom, calls=%fused_computation.1 | custom fusion | bytes 6291552 | tf_op jit(solution)/shard_map/while/body/eval_jaxpr/gather | solution.py:25
  94.3 8.9 %reshape.95 = bf16[4,768,8,64]{3,2,1,0:T(8,128)(2,1)} reshape(bf16[24,128,512]{2,1,0:T(8,128)(2,1)} %gather_fusion.1) | data formatting | bytes 6291456 | tf_op jit(solution)/shard_map/while/body/eval_jaxpr/reshape | solution.py:25
  103.2 15.6 %fusion.17 = bf16[4,128,8,64]{1,3,2,0:T(8,128)(2,1)S(1)} fusion(f32[4,8,128]{2,1,0:T(8,128)S(1)} %fusion.30, bf16[4,768,8,64]{3,2,1,0:T(8,128)(2,1)} %reshape.95, pred[4]{0:T(512)(128)(4,1)S(1)} %iota_compare_fusion, f32[4,8,768,128]{3,2,1,0:T(8,128)} %fusion.6), kind=kOutput, calls=%fused_computation.20 | convolution fusion | flops 418910976 | bytes 16269316 | tf_op jit(solution)/shard_map/while/body/eval_jaxpr/qhij,qjhd->qihd/dot_general | solution.py:31
  118.8 0.6 copy.38
  119.4 1.4 %reshape.98 = bf16[512,512]{1,0:T(8,128)(2,1)} reshape(bf16[4,128,8,64]{3,2,1,0:T(8,128)(2,1)S(1)} %copy.38) | data formatting | bytes 1048576 | tf_op jit(solution)/shard_map/reshape | solution.py:58
  (4 shorter events, 0.0 us)
Async XLA Ops:
  0.0 54.8 %copy-start.1 = (bf16[512,512]{1,0:T(8,128)(2,1)S(1)}, bf16[512,512]{1,0:T(8,128)(2,1)}, u32[]{:S(2)}) copy-start(bf16[512,512]{1,0:T(8,128)(2,1)} %param.7) | copy-start | bytes 1572868
  0.0 54.8 %copy-start = (bf16[512,512]{1,0:T(8,128)(2,1)S(1)}, bf16[512,512]{1,0:T(8,128)(2,1)}, u32[]{:S(2)}) copy-start(bf16[512,512]{1,0:T(8,128)(2,1)} %param.8) | copy-start | bytes 1572868
  1.4 50.4 %collective-permute-start.2 = (bf16[2,4,128,512]{3,2,0,1:T(8,128)(2,1)S(1)}, bf16[2,4,128,512]{3,2,0,1:T(8,128)(2,1)}, u32[]{:S(2)}, u32[]{:S(2)}) collective-permute-start(bf16[2,4,128,512]{3,2,0,1:T(8,128)(2,1)S(1)} %pad_maximum_fusion.1), channel_id=1, source_target_pairs={{64,0},{0,64},{65,1},{1,65},{66,2},{2,66},{67,3},{3,67},{68,4},{4,... | collective-permute-start | bytes 3145736 | tf_op jit(solution)/shard_map/ppermute | solution.py:16
  8.2 46.6 %collective-permute-start = (bf16[2,512,512]{2,1,0:T(8,128)(2,1)}, bf16[2,512,512]{2,1,0:T(8,128)(2,1)}, u32[]{:S(2)}, u32[]{:S(2)}) collective-permute-start(bf16[2,512,512]{2,1,0:T(8,128)(2,1)} %pad_maximum_fusion.2), channel_id=1, source_target_pairs={{63,0},{0,1},{1,2},{2,3},{3,4},{4,5},{5,6},{6,7},{7,8},{8,9},{9,10... | collective-permute-start | bytes 3145736 | tf_op jit(solution)/shard_map/ppermute | solution.py:16
  9.8 45.0 %collective-permute-start.1 = (bf16[2,512,512]{2,1,0:T(8,128)(2,1)}, bf16[2,512,512]{2,1,0:T(8,128)(2,1)}, u32[]{:S(2)}, u32[]{:S(2)}) collective-permute-start(bf16[2,512,512]{2,1,0:T(8,128)(2,1)} %pad_maximum_fusion.2), channel_id=1, source_target_pairs={{1,0},{2,1},{3,2},{4,3},{5,4},{6,5},{7,6},{8,7},{9,8},{10,9},{11,1... | collective-permute-start | bytes 3145736 | tf_op jit(solution)/shard_map/ppermute | solution.py:16
  9.8 42.0 %collective-permute-start.3 = (s32[1,4]{1,0:T(1,128)}, s32[1,4]{1,0:T(1,128)S(1)}, u32[]{:S(2)}, u32[]{:S(2)}) collective-permute-start(s32[1,4]{1,0:T(1,128)} %param.11), channel_id=1, source_target_pairs={{64,0},{0,64},{65,1},{1,65},{66,2},{2,66},{67,3},{3,67},{68,4},{4,... | collective-permute-start | bytes 56 | tf_op jit(solution)/shard_map/ppermute | solution.py:16
where the time goes:
time: 121 us
  waiting for transfers between devices  38.1 us (31%)
  local copies, waits for them, and re-layouts  32.7 us (27%)
  matrix products  24.8 us (20%)
  other arithmetic  17.5 us (14%)
  starting transfers between devices  6.95 us (6%)
    ppermute x4, waiting for transfers between devices, shifted(): return lax.ppermute(block, axis, route)  38.1 us
    dot_general x1, matrix products, attend_block(): jnp.einsum('qhij,qjhd->qihd', weights, value_set, preferred_element_type=...  15.6 us
    sub x1, other arithmetic, attend_block(): weights = jax.nn.softmax(scores, axis=-1).astype(jnp.bfloat16)  11.1 us
    dot_general x1, matrix products, attend_block(): jnp.einsum('qihd,qjhd->qhij', query_set, key_set, preferred_element_type=...  9.15 us
    reshape x1, local copies, waits for them, and re-layouts, attend_block(): value_set = pool[1][lists].reshape(BLOCK, listed * tile, HEADS, HEAD_DIM)  8.92 us
    reshape x1, local copies, waits for them, and re-layouts, attend_block(): key_set = pool[0][lists].reshape(BLOCK, listed * tile, HEADS, HEAD_DIM)  8.91 us
    ppermute x4, starting transfers between devices, shifted(): return lax.ppermute(block, axis, route)  6.95 us
    gather x1, local copies, waits for them, and re-layouts, attend_block(): key_set = pool[0][lists].reshape(BLOCK, listed * tile, HEADS, HEAD_DIM)  4.11 us
  transfers between devices with their start and end apart: 4, of which 1 were waited for; matrix products, arithmetic and copies ran while one was open for 6% of the time, Pallas kernels for 0%

commit v1 on v0

v1 whole, which is shorter than its diff:
```python
import math

import jax
import jax.numpy as jnp
from jax import lax
from jax.experimental import pallas as pl
from jax.experimental.pallas import tpu as pltpu
from jax.sharding import PartitionSpec as P


HEADS = 8
HEAD_DIM = 64
TILE = 128
TILES = 4
LISTED = 6
PAIRS = 4
BATCH = 4
WIDTH = HEADS * HEAD_DIM
AXES = ("group", "slab")
SCALE = HEAD_DIM ** (-0.5) * math.log2(math.e)
LOWEST = -1e30

VMEM = pl.BlockSpec(memory_space=pltpu.VMEM)
SMEM = pl.BlockSpec(memory_space=pltpu.SMEM)


def move(block, target):
    groups, slabs = lax.axis_size("group"), lax.axis_size("slab")
    route = []
    for g in range(groups):
        for s in range(slabs):
            to_g, to_s = target(g, s)
            route.append((g * slabs + s, (to_g % groups) * slabs + to_s % slabs))
    return lax.ppermute(block, AXES, route)


def to_chip(g, s):
    return g, s ^ 1


def to_cross(g, s):
    return g, s ^ 3


def to_forward(g, s):
    return 1 - g, s ^ 3


def to_along(g, s):
    return g, (s + 4 if s % 2 == 0 else s - 4)


def to_group(g, s):
    return 1 - g, s


def prepare_kernel(q_ref, v_ref, w_ref, v_out):
    for t in range(TILES):
        rows = pl.ds(t * TILE, TILE)
        for p in range(PAIRS):
            lanes = pl.ds(p * TILE, TILE)
            v_out[rows, lanes] = v_ref[rows, lanes].T
            qt = q_ref[rows, lanes].T
            zero = jnp.zeros((HEAD_DIM, TILE), jnp.bfloat16)
            w_ref[t, p, :HEAD_DIM, :TILE] = qt[:HEAD_DIM]
            w_ref[t, p, :HEAD_DIM, TILE:] = zero
            w_ref[t, p, HEAD_DIM:, :TILE] = zero
            w_ref[t, p, HEAD_DIM:, TILE:] = qt[HEAD_DIM:]


def prepare(q, v):
    return pl.pallas_call(
        prepare_kernel,
        out_shape=(
            jax.ShapeDtypeStruct((TILES, PAIRS, TILE, 2 * TILE), jnp.bfloat16),
            jax.ShapeDtypeStruct(v.shape, jnp.bfloat16),
        ),
        in_specs=[VMEM, VMEM],
        out_specs=(VMEM, VMEM),
        compiler_params=pltpu.CompilerParams(vmem_limit_bytes=8 << 20),
        cost_estimate=pl.CostEstimate(flops=10**6, bytes_accessed=3 << 20, transcendentals=0),
        name="prepare",
    )(q, v)


def list_items(lists_ref, live, source_of, items):
    count = jnp.int32(0)
    for t in range(TILES):
        for j in range(LISTED):
            here, tile = source_of(lists_ref[t, j])
            items[count] = t * 16 + tile
            count = count + jnp.where(jnp.logical_and(here, t < live), 1, 0)
    for j in range(BATCH - 1):
        items[count + j] = TILES * 16
    return lax.div(count + (BATCH - 1), jnp.int32(BATCH))


def attend_items(batches, items, k_ref, v_ref, w_ref, acc, peak, total):
    def batch(b, carry):
        for u in range(BATCH):
            item = items[b * BATCH + u]
            t = lax.div(item, jnp.int32(16))
            rows = pl.ds(pl.multiple_of(lax.rem(item, jnp.int32(16)) * TILE, TILE), TILE)
            tq = jnp.minimum(t, TILES - 1)
            tops, sums, mixes = [], [], []
            for p in range(PAIRS):
                lanes = pl.ds(p * TILE, TILE)
                scores = jnp.dot(k_ref[rows, lanes], w_ref[tq, p], preferred_element_type=jnp.float32)
                top = jnp.max(scores, axis=0, keepdims=True)
                weights = jnp.exp2(scores * SCALE - top * SCALE)
                add = jnp.sum(weights, axis=0, keepdims=True)
                weights = weights.astype(jnp.bfloat16)
                vt = v_ref[rows, lanes]
                for h in range(2):
                    half = slice(h * TILE, (h + 1) * TILE)
                    tops.append(top[:, half])
                    sums.append(add[:, half])
                    mixes.append(
                        jnp.dot(
                            vt[h * HEAD_DIM : (h + 1) * HEAD_DIM],
                            weights[:, half],
                            preferred_element_type=jnp.float32,
                        )
                    )
            top = jnp.concatenate(tops, axis=0)
            add = jnp.concatenate(sums, axis=0)
            old = peak[t]
            new = jnp.maximum(old, top)
            keep = jnp.exp2((old - new) * SCALE)
            take = jnp.exp2((top - new) * SCALE)
            peak[t] = new
            total[t] = total[t] * keep + add * take
            for h in range(HEADS):
                dims = pl.ds(h * HEAD_DIM, HEAD_DIM)
                acc[t, dims] = acc[t, dims] * keep[h : h + 1] + mixes[h] * take[h : h + 1]
        return carry

    lax.fori_loop(0, batches, batch, 0)


def first_kernel(lists, live, k_ref, v_ref, w_ref, acc, peak, total, items):
    acc[...] = jnp.zeros_like(acc)
    peak[...] = jnp.full_like(peak, LOWEST)
    total[...] = jnp.zeros_like(total)
    batches = list_items(lists, live[0], lambda pos: (pos < TILES, lax.rem(pos, 4)), items)
    attend_items(batches, items, k_ref, v_ref, w_ref, acc, peak, total)


STATE = (
    jax.ShapeDtypeStruct((TILES + 1, WIDTH, TILE), jnp.float32),
    jax.ShapeDtypeStruct((TILES + 1, HEADS, TILE), jnp.float32),
    jax.ShapeDtypeStruct((TILES + 1, HEADS, TILE), jnp.float32),
)
ITEMS = pltpu.SMEM((TILES * LISTED + BATCH,), jnp.int32)


def flops(items):
    return pl.CostEstimate(flops=items * 40_000_000, bytes_accessed=1 << 20, transcendentals=0)


def first_stage(lists, live, k, v, w):
    return pl.pallas_call(
        first_kernel,
        out_shape=STATE,
        in_specs=[SMEM, SMEM] + [VMEM] * 3,
        out_specs=(VMEM,) * 3,
        scratch_shapes=[ITEMS],
        compiler_params=pltpu.CompilerParams(vmem_limit_bytes=16 << 20),
        cost_estimate=flops(8),
        name="first_stage",
    )(lists, live, k, v, w)


def pool_half(half, odd):
    def source_of(ids_ref):
        def find(pos):
            other = jnp.where(odd, 2 * TILES, TILES)
            beside = pos - other
            is_beside = jnp.logical_and(beside >= 2 * half, beside < 2 * half + 2)
            far = ids_ref[0, jnp.maximum(pos - 3 * TILES, 0)] - 2 * half
            is_far = jnp.logical_and(pos >= 3 * TILES, jnp.logical_and(far >= 0, far < 2))
            tile = jnp.where(is_beside, beside - 2 * half, jnp.where(is_far, far + 2, 0))
            return jnp.logical_or(is_beside, is_far), tile

        return find

    return source_of


def pick(inner, refs, k_all, v_all):
    kb, vb, kd, vd, kc, vc = refs

    @pl.when(inner)
    def _():
        k_all[: 2 * TILE] = kb[...]
        v_all[: 2 * TILE] = vb[...]

    @pl.when(jnp.logical_not(inner))
    def _():
        k_all[: 2 * TILE] = kd[...]
        v_all[: 2 * TILE] = vd[...]

    k_all[2 * TILE :] = kc[...]
    v_all[2 * TILE :] = vc[...]


def middle_kernel(lists, live, ids, slab, kn, vn, kb, vb, kd, vd, kc, vc, w_ref, acc0, peak0, total0, acc, peak, total, items, k_all, v_all):
    odd = lax.rem(slab[0], 2) == 1
    inner = jnp.logical_or(lax.rem(slab[0], 4) == 1, lax.rem(slab[0], 4) == 2)

    def near(pos):
        at = pos - jnp.where(odd, TILES, 2 * TILES)
        here = jnp.logical_and(at >= 0, at < TILES)
        return here, jnp.where(here, at, 0)

    batches = list_items(lists, live[0], near, items)
    attend_items(batches, items, kn, vn, w_ref, acc, peak, total)
    pick(inner, (kb, vb, kd, vd, kc, vc), k_all, v_all)
    batches = list_items(lists, live[0], pool_half(0, odd)(ids), items)
    attend_items(batches, items, k_all, v_all, w_ref, acc, peak, total)


def middle_stage(lists, live, ids, slab, tiles, w, state):
    return pl.pallas_call(
        middle_kernel,
        out_shape=STATE,
        in_specs=[SMEM] * 4 + [VMEM] * 12,
        out_specs=(VMEM,) * 3,
        input_output_aliases={13: 0, 14: 1, 15: 2},
        scratch_shapes=[ITEMS, pltpu.VMEM((4 * TILE, WIDTH), jnp.bfloat16), pltpu.VMEM((4 * TILE, WIDTH), jnp.bfloat16)],
        compiler_params=pltpu.CompilerParams(vmem_limit_bytes=20 << 20),
        cost_estimate=flops(16),
        name="middle_stage",
    )(lists, live, ids, slab, *tiles, w, *state)


def last_kernel(lists, live, ids, slab, kb, vb, kd, vd, kc, vc, w_ref, acc, peak, total, out, items, k_all, v_all):
    odd = lax.rem(slab[0], 2) == 1
    inner = jnp.logical_or(lax.rem(slab[0], 4) == 1, lax.rem(slab[0], 4) == 2)
    pick(inner, (kb, vb, kd, vd, kc, vc), k_all, v_all)
    batches = list_items(lists, live[0], pool_half(1, odd)(ids), items)
    attend_items(batches, items, k_all, v_all, w_ref, acc, peak, total)
    for t in range(TILES):
        rows = pl.ds(t * TILE, TILE)

        @pl.when(t < live[0])
        def _():
            share = 1.0 / total[t]
            for p in range(PAIRS):
                halves = [
                    acc[t, pl.ds((2 * p + h) * HEAD_DIM, HEAD_DIM)] * share[2 * p + h : 2 * p + h + 1]
                    for h in range(2)
                ]
                mixed = jnp.concatenate(halves, axis=0).astype(jnp.bfloat16)
                out[rows, pl.ds(p * TILE, TILE)] = mixed.T

        @pl.when(t >= live[0])
        def _():
            out[rows] = jnp.zeros((TILE, WIDTH), jnp.bfloat16)


def last_stage(lists, live, ids, slab, tiles, w, state):
    return pl.pallas_call(
        last_kernel,
        out_shape=jax.ShapeDtypeStruct((TILES * TILE, WIDTH), jnp.bfloat16),
        in_specs=[SMEM] * 4 + [VMEM] * 10,
        out_specs=VMEM,
        scratch_shapes=[ITEMS, pltpu.VMEM((4 * TILE, WIDTH), jnp.bfloat16), pltpu.VMEM((4 * TILE, WIDTH), jnp.bfloat16)],
        compiler_params=pltpu.CompilerParams(vmem_limit_bytes=20 << 20),
        cost_estimate=flops(8),
        name="last_stage",
    )(lists, live, ids, slab, *tiles, w, *state)


def shards(queries, keys, values, neighbours, live_tiles, boundary_ids):
    half = 2 * TILE
    slab = lax.axis_index("slab").astype(jnp.int32)[None]
    ka, kz = keys[:half], keys[half:]
    w, vt = prepare(queries, values)
    va, vz = vt[:half], vt[half:]
    near = move(keys, to_chip), move(vt, to_chip)
    cross = [move(x, to_cross) for x in (ka, va, kz, vz)]
    far_last = move(vz, to_group)
    ids = move(boundary_ids, to_group)
    far = [move(cross[i], to_forward) for i in range(3)] + [far_last]
    along = [move(cross[i], to_along) for i in range(4)]
    state = first_stage(neighbours, live_tiles, keys, vt, w)
    tiles = (*near, cross[0], cross[1], along[0], along[1], far[0], far[1])
    state = middle_stage(neighbours, live_tiles, ids, slab, tiles, w, state)
    tiles = (cross[2], cross[3], along[2], along[3], far[2], far[3])
    return last_stage(neighbours, live_tiles, ids, slab, tiles, w, state)


def solution(mesh):
    spec = P(AXES, None)
    return jax.shard_map(
        shards,
        mesh=mesh,
        in_specs=(spec, spec, spec, spec, P(AXES), spec),
        out_specs=spec,
        check_vma=False,
    )
```

time: 121 us -> 68.1 us (0.56)
  local copies, waits for them, and re-layouts: 32.7 us -> 7.18 us
  matrix products: 24.8 us -> 0 us
  starting transfers between devices: 6.95 us -> 27 us
  other arithmetic: 17.5 us -> 0 us
  waiting for transfers between devices: 38.1 us -> 23.8 us
  Pallas kernels: 0 us -> 8.15 us
    dot_general x2 -> x0, matrix products: 24.8 us -> none  [the longest x1 15.6 us: attend_block(): jnp.einsum('qhij,qjhd->qihd', weights, value_set, preferred_element_type=...]
    ppermute x4 -> x15, starting transfers between devices: 6.95 us -> 27 us  [move(): return lax.ppermute(block, AXES, route)]
    reshape x4 -> x0, local copies, waits for them, and re-layouts: 19.8 us -> none  [the longest x1 8.92 us: attend_block(): value_set = pool[1][lists].reshape(BLOCK, listed * tile, HEADS, HEAD_DIM)]
    ppermute x4 -> x15, waiting for transfers between devices: 38.1 us -> 23.8 us  [move(): return lax.ppermute(block, AXES, route)]
    sub x1 -> x0, other arithmetic: 11.1 us -> none  [attend_block(): weights = jax.nn.softmax(scores, axis=-1).astype(jnp.bfloat16)]
    gather x3 -> x0, local copies, waits for them, and re-layouts: 8.24 us -> none  [the longest x1 4.11 us: attend_block(): key_set = pool[0][lists].reshape(BLOCK, listed * tile, HEADS, HEAD_DIM)]
    pallas_call x0 -> x4, Pallas kernels: none -> 8.15 us  [the longest x1 3.47 us: last_stage(): pl.pallas_call(last_kernel, out_shape=jax.ShapeDtypeStruct((TILES * TILE,...]
    unnamed x4 -> x34, local copies, waits for them, and re-layouts: 0.01 us -> 6.41 us
  transfers between devices with their start and end apart: 4 -> 15, of which waited for: 1 -> 4; matrix products, arithmetic and copies ran while one was open for 6% -> 0% of each run, Pallas kernels for 0% -> 6%
where the time goes in v1:
time: 68.1 us; the launch traced here: 67 us
  starting transfers between devices  27 us (40%)
  waiting for transfers between devices  23.8 us (35%)
  Pallas kernels  8.15 us (12%)
  local copies, waits for them, and re-layouts  7.18 us (11%)
  between operations  0.86 us (1%)
    ppermute x15, starting transfers between devices, move(): return lax.ppermute(block, AXES, route)  27 us
    ppermute x15, waiting for transfers between devices, move(): return lax.ppermute(block, AXES, route)  23.8 us
    unnamed x34, local copies, waits for them, and re-layouts  6.41 us
    pallas_call x1, Pallas kernels, last_stage(): pl.pallas_call(last_kernel, out_shape=jax.ShapeDtypeStruct((TILES * TILE,...  3.47 us
    pallas_call x1, Pallas kernels, middle_stage(): pl.pallas_call(middle_kernel, out_shape=STATE, in_specs=[SMEM] * 4 + [VME...  2.74 us
    pallas_call x1, Pallas kernels, first_stage(): pl.pallas_call(first_kernel, out_shape=STATE, in_specs=[SMEM, SMEM] + [VM...  1.58 us
  transfers between devices with their start and end apart: 15, of which 4 were waited for; matrix products, arithmetic and copies ran while one was open for 0% of the time, Pallas kernels for 6%

profile of v1, /device:TPU:1, one launch (start us, length us, event | category | flops | bytes accessed | tf_op | source)
XLA Modules:
  0.0 67.0 jit_solution(7258323954050264432)
XLA Ops:
  0.0 0.0 copy-start
  0.0 0.0 copy-start.1
  0.0 1.1 %copy-done.1 = bf16[512,512]{1,0:T(8,128)(2,1)S(1)} copy-done((bf16[512,512]{1,0:T(8,128)(2,1)S(1)}, bf16[512,512]{1,0:T(8,128)(2,1)}, u32[]{:S(2)}) %copy-start.1) | copy-done | bytes 524312
  1.1 0.0 copy-start.2
  1.1 1.0 %copy-done.2 = bf16[512,512]{1,0:T(8,128)(2,1)S(1)} copy-done((bf16[512,512]{1,0:T(8,128)(2,1)S(1)}, bf16[512,512]{1,0:T(8,128)(2,1)}, u32[]{:S(2)}) %copy-start.2) | copy-done | bytes 524312
  2.1 0.4 prepare.1
  2.5 0.0 copy-start.16
  2.5 0.0 copy-start.15
  2.5 0.7 %fusion = (bf16[256,512]{1,0:T(8,128)(2,1)S(1)}, bf16[256,512]{1,0:T(8,128)(2,1)}) fusion(bf16[512,512]{1,0:T(8,128)(2,1)S(1)} %get-tuple-element.13.v_ref), kind=kLoop, calls=%fused_computation | loop fusion | bytes 1048576 | tf_op jit(solution)/shard_map/slice | solution.py:280
  3.3 3.0 %collective-permute-start.10 = (bf16[256,512]{1,0:T(8,128)(2,1)S(1)}, bf16[256,512]{1,0:T(8,128)(2,1)S(1)}, u32[]{:S(2)}, u32[]{:S(2)}) collective-permute-start(bf16[256,512]{1,0:T(8,128)(2,1)S(1)} %get-tuple-element.21), channel_id=1, source_target_pairs={{0,3},{1,2},{2,1},{3,0},{4,7},{5,6},{6,5},{7,4},{8,11},{9,10},{10,... | collective-permute-start | bytes 786440 | tf_op jit(solution)/shard_map/ppermute | solution.py:34
  6.3 0.0 copy-done
  6.3 0.1 collective-permute-start.9
  6.4 0.1 collective-permute-start.8
  6.5 1.6 %collective-permute-start.2 = (bf16[256,512]{1,0:T(8,128)(2,1)}, bf16[256,512]{1,0:T(8,128)(2,1)S(1)}, u32[]{:S(2)}, u32[]{:S(2)}) collective-permute-start(bf16[256,512]{1,0:T(8,128)(2,1)} %get-tuple-element.22), channel_id=1, source_target_pairs={{0,3},{1,2},{2,1},{3,0},{4,7},{5,6},{6,5},{7,4},{8,11},{9,10},{10,... | collective-permute-start | bytes 786440 | tf_op jit(solution)/shard_map/ppermute | solution.py:34
  8.2 0.0 copy-done.16
  8.2 3.3 %collective-permute-start = (s32[1,4]{1,0:T(1,128)S(1)}, s32[1,4]{1,0:T(1,128)S(1)}, u32[]{:S(2)}, u32[]{:S(2)}) collective-permute-start(s32[1,4]{1,0:T(1,128)S(1)} %copy-done.16), channel_id=1, source_target_pairs={{0,64},{1,65},{2,66},{3,67},{4,68},{5,69},{6,70},{7,71},{8,72},{9,... | collective-permute-start | bytes 56 | tf_op jit(solution)/shard_map/ppermute | solution.py:34
  11.5 15.9 %collective-permute-done.ids = s32[1,4]{1,0:T(1,128)S(1)} collective-permute-done((s32[1,4]{1,0:T(1,128)S(1)}, s32[1,4]{1,0:T(1,128)S(1)}, u32[]{:S(2)}, u32[]{:S(2)}) %collective-permute-start) | collective-permute-done | bytes 48 | tf_op jit(solution)/shard_map/ppermute | solution.py:34
  27.4 0.1 collective-permute-start.1
  27.5 0.0 collective-permute-done.10.vb
  27.5 4.9 %collective-permute-start.12 = (bf16[256,512]{1,0:T(8,128)(2,1)S(1)}, bf16[256,512]{1,0:T(8,128)(2,1)S(1)}, u32[]{:S(2)}, u32[]{:S(2)}) collective-permute-start(bf16[256,512]{1,0:T(8,128)(2,1)S(1)} %collective-permute-done.10.vb), channel_id=1, source_target_pairs={{0,4},{1,61},{2,6},{3,63},{4,8},{5,1},{6,10},{7,3},{8,12},{9,5},{1... | collective-permute-start | bytes 786440 | tf_op jit(solution)/shard_map/ppermute | solution.py:34
  32.4 0.0 collective-permute-done.9.kb
  32.4 0.0 collective-permute-start.7
  32.4 0.0 collective-permute-done.2.vb
  32.4 0.8 %collective-permute-start.14 = (bf16[256,512]{1,0:T(8,128)(2,1)S(1)}, bf16[256,512]{1,0:T(8,128)(2,1)S(1)}, u32[]{:S(2)}, u32[]{:S(2)}) collective-permute-start(bf16[256,512]{1,0:T(8,128)(2,1)S(1)} %collective-permute-done.10.vb), channel_id=1, source_target_pairs={{0,67},{1,66},{2,65},{3,64},{4,71},{5,70},{6,69},{7,68},{8,75},{9,... | collective-permute-start | bytes 786440 | tf_op jit(solution)/shard_map/ppermute | solution.py:34
  33.3 0.0 copy-start.3
  33.3 0.7 %copy-done.3 = bf16[256,512]{1,0:T(8,128)(2,1)} copy-done((bf16[256,512]{1,0:T(8,128)(2,1)}, bf16[256,512]{1,0:T(8,128)(2,1)S(1)}, u32[]{:S(2)}) %copy-start.3) | copy-done | bytes 262168
  34.0 2.4 %collective-permute-done.1.kb = bf16[256,512]{1,0:T(8,128)(2,1)} collective-permute-done((bf16[256,512]{1,0:T(8,128)(2,1)S(1)}, bf16[256,512]{1,0:T(8,128)(2,1)}, u32[]{:S(2)}, u32[]{:S(2)}) %collective-permute-start.1) | collective-permute-done | bytes 262176 | tf_op jit(solution)/shard_map/ppermute | solution.py:34
  36.4 4.9 %collective-permute-start.11 = (bf16[256,512]{1,0:T(8,128)(2,1)S(1)}, bf16[256,512]{1,0:T(8,128)(2,1)S(1)}, u32[]{:S(2)}, u32[]{:S(2)}) collective-permute-start(bf16[256,512]{1,0:T(8,128)(2,1)S(1)} %collective-permute-done.9.kb), channel_id=1, source_target_pairs={{0,4},{1,61},{2,6},{3,63},{4,8},{5,1},{6,10},{7,3},{8,12},{9,5},{1... | collective-permute-start | bytes 786440 | tf_op jit(solution)/shard_map/ppermute | solution.py:34
  41.3 0.0 collective-permute-done.12.vd
  41.3 0.7 %copy-done.7 = bf16[256,512]{1,0:T(8,128)(2,1)} copy-done((bf16[256,512]{1,0:T(8,128)(2,1)}, bf16[256,512]{1,0:T(8,128)(2,1)S(1)}, u32[]{:S(2)}) %copy-start.7) | copy-done | bytes 262168
  42.0 0.0 collective-permute-start.13
  42.0 0.7 %copy-done.5 = bf16[256,512]{1,0:T(8,128)(2,1)} copy-done((bf16[256,512]{1,0:T(8,128)(2,1)}, bf16[256,512]{1,0:T(8,128)(2,1)S(1)}, u32[]{:S(2)}) %copy-start.5) | copy-done | bytes 262168
  42.7 0.0 collective-permute-done.14.vc
  42.7 0.7 %copy-done.9 = bf16[256,512]{1,0:T(8,128)(2,1)} copy-done((bf16[256,512]{1,0:T(8,128)(2,1)}, bf16[256,512]{1,0:T(8,128)(2,1)S(1)}, u32[]{:S(2)}) %copy-start.9) | copy-done | bytes 262168
  43.4 0.1 collective-permute-start.6
  43.5 0.0 collective-permute-done.8.vn
  43.5 1.2 %collective-permute-start.4 = (bf16[256,512]{1,0:T(8,128)(2,1)S(1)}, bf16[256,512]{1,0:T(8,128)(2,1)}, u32[]{:S(2)}, u32[]{:S(2)}) collective-permute-start(bf16[256,512]{1,0:T(8,128)(2,1)S(1)} %collective-permute-done.2.vb), channel_id=1, source_target_pairs={{0,4},{1,61},{2,6},{3,63},{4,8},{5,1},{6,10},{7,3},{8,12},{9,5},{1... | collective-permute-start | bytes 786440 | tf_op jit(solution)/shard_map/ppermute | solution.py:34
  44.8 0.0 collective-permute-done.11.kd
  44.8 0.7 %copy-done.11 = bf16[256,512]{1,0:T(8,128)(2,1)} copy-done((bf16[256,512]{1,0:T(8,128)(2,1)}, bf16[256,512]{1,0:T(8,128)(2,1)S(1)}, u32[]{:S(2)}) %copy-start.11) | copy-done | bytes 262168
  45.5 5.1 %collective-permute-start.3 = (bf16[256,512]{1,0:T(8,128)(2,1)}, bf16[256,512]{1,0:T(8,128)(2,1)}, u32[]{:S(2)}, u32[]{:S(2)}) collective-permute-start(bf16[256,512]{1,0:T(8,128)(2,1)} %collective-permute-done.1.kb), channel_id=1, source_target_pairs={{0,4},{1,61},{2,6},{3,63},{4,8},{5,1},{6,10},{7,3},{8,12},{9,5},{1... | collective-permute-start | bytes 786440 | tf_op jit(solution)/shard_map/ppermute | solution.py:34
  50.6 4.5 %collective-permute-done.13.kc = bf16[256,512]{1,0:T(8,128)(2,1)S(1)} collective-permute-done((bf16[256,512]{1,0:T(8,128)(2,1)S(1)}, bf16[256,512]{1,0:T(8,128)(2,1)S(1)}, u32[]{:S(2)}, u32[]{:S(2)}) %collective-permute-start.13) | collective-permute-done | bytes 262176 | tf_op jit(solution)/shard_map/ppermute | solution.py:34
  55.0 0.7 %copy-done.13 = bf16[256,512]{1,0:T(8,128)(2,1)} copy-done((bf16[256,512]{1,0:T(8,128)(2,1)}, bf16[256,512]{1,0:T(8,128)(2,1)S(1)}, u32[]{:S(2)}) %copy-start.13) | copy-done | bytes 262168
  55.7 1.7 %collective-permute-start.5 = (bf16[256,512]{1,0:T(8,128)(2,1)}, bf16[256,512]{1,0:T(8,128)(2,1)}, u32[]{:S(2)}, u32[]{:S(2)}) collective-permute-start(bf16[256,512]{1,0:T(8,128)(2,1)} %collective-permute-done.1.kb), channel_id=1, source_target_pairs={{0,67},{1,66},{2,65},{3,64},{4,71},{5,70},{6,69},{7,68},{8,75},{9,... | collective-permute-start | bytes 786440 | tf_op jit(solution)/shard_map/ppermute | solution.py:34
  58.1 0.0 copy-start.4
  58.1 0.0 copy-start.6
  58.1 0.0 copy-start.8
  58.1 0.0 copy-start.10
  58.1 0.0 copy-start.12
  58.1 0.0 copy-start.14
  58.1 0.0 copy-done.15
  58.1 1.6 %first_stage.1 = (f32[5,512,128]{2,1,0:T(8,128)S(1)}, f32[5,8,128]{2,1,0:T(8,128)S(1)}, f32[5,8,128]{2,1,0:T(8,128)S(1)}) custom-call(s32[4,6]{1,0:T(4,128)S(1)} %copy-done.15, s32[1]{0:T(128)S(6)} %copy.13.live, bf16[512,512]{1,0:T(8,128)(2,1)S(1)} %copy-done, bf16[512,512]{1,0:T(8,128)(2,1)S(1)} %get-tuple-element.13.v_ref, ...), custom_call_target="tpu_custom_call" | custom-call | flops 320000000 | bytes 1048576 | tf_op jit(solution)/shard_map/first_stage/pallas_call | solution.py:162
  59.7 0.0 collective-permute-done.7.kn
  59.7 0.0 copy-done.4
  59.7 0.0 copy-done.6
  59.7 0.0 copy-done.8
  59.8 0.0 copy-done.10
  59.8 0.0 copy-done.12
  59.8 0.0 copy-done.14
  59.8 2.7 %middle_stage.1 = (f32[5,512,128]{2,1,0:T(8,128)S(1)}, f32[5,8,128]{2,1,0:T(8,128)S(1)}, f32[5,8,128]{2,1,0:T(8,128)S(1)}) custom-call(s32[4,6]{1,0:T(4,128)S(1)} %copy-done.15, s32[1]{0:T(128)S(6)} %copy.13.live, s32[1,4]{1,0:T(1,128)S(1)} %collective-permute-done.ids, s32[1]{0:T(128)} %bitcast.slab, ...), custom_call_target="tpu_custom_call", output_to_operand_aliasing={{0}: (13, {}), {1}: (14, {}), {2}: (15, {})} | custom-call | flops 640000000 | bytes 1048576 | tf_op jit(solution)/shard_map/middle_stage/pallas_call | solution.py:224
  62.5 0.0 collective-permute-done.6.vc
  62.5 0.0 collective-permute-done.4.vd
  62.6 0.0 collective-permute-done.3.kd
  62.6 0.9 %collective-permute-done.5.kc = bf16[256,512]{1,0:T(8,128)(2,1)} collective-permute-done((bf16[256,512]{1,0:T(8,128)(2,1)}, bf16[256,512]{1,0:T(8,128)(2,1)}, u32[]{:S(2)}, u32[]{:S(2)}) %collective-permute-start.5) | collective-permute-done | bytes 262176 | tf_op jit(solution)/shard_map/ppermute | solution.py:34
  63.5 3.5 %last_stage.1 = bf16[512,512]{1,0:T(8,128)(2,1)} custom-call(s32[4,6]{1,0:T(4,128)S(1)} %copy-done.15, s32[1]{0:T(128)S(6)} %copy.13.live, s32[1,4]{1,0:T(1,128)S(1)} %collective-permute-done.ids, s32[1]{0:T(128)} %bitcast.slab, bf16[256,512]{1,0:T(8,128)(2,1)} %collective-permute-done.1.kb, bf16[256,512]{1,0:T(8,128)(2,1)S(1)} %collective-permute-done.2.vb, ...), custom_call_target="tpu_custom_call" | custom-call | flops 320000000 | bytes 1048576 | tf_op jit(solution)/shard_map/last_stage/pallas_call | solution.py:263
  (6 shorter events, 0.0 us)
Async XLA Ops:
  0.0 6.3 %copy-start = (bf16[512,512]{1,0:T(8,128)(2,1)S(1)}, bf16[512,512]{1,0:T(8,128)(2,1)}, u32[]{:S(2)}) copy-start(bf16[512,512]{1,0:T(8,128)(2,1)} %k_ref.1) | copy-start | bytes 1572868
  0.0 1.1 %copy-start.1 = (bf16[512,512]{1,0:T(8,128)(2,1)S(1)}, bf16[512,512]{1,0:T(8,128)(2,1)}, u32[]{:S(2)}) copy-start(bf16[512,512]{1,0:T(8,128)(2,1)} %q_ref.1) | copy-start | bytes 1572868
  1.1 1.0 %copy-start.2 = (bf16[512,512]{1,0:T(8,128)(2,1)S(1)}, bf16[512,512]{1,0:T(8,128)(2,1)}, u32[]{:S(2)}) copy-start(bf16[512,512]{1,0:T(8,128)(2,1)} %v_ref.1) | copy-start | bytes 1572868
  2.5 5.7 %copy-start.16 = (s32[1,4]{1,0:T(1,128)S(1)}, s32[1,4]{1,0:T(1,128)}, u32[]{:S(2)}) copy-start(s32[1,4]{1,0:T(1,128)} %param.11) | copy-start | bytes 52
  2.5 55.6 %copy-start.15 = (s32[4,6]{1,0:T(4,128)S(1)}, s32[4,6]{1,0:T(4,128)}, u32[]{:S(2)}) copy-start(s32[4,6]{1,0:T(4,128)} %lists.5) | copy-start | bytes 292
  3.3 24.2 %collective-permute-start.10 = (bf16[256,512]{1,0:T(8,128)(2,1)S(1)}, bf16[256,512]{1,0:T(8,128)(2,1)S(1)}, u32[]{:S(2)}, u32[]{:S(2)}) collective-permute-start(bf16[256,512]{1,0:T(8,128)(2,1)S(1)} %get-tuple-element.21), channel_id=1, source_target_pairs={{0,3},{1,2},{2,1},{3,0},{4,7},{5,6},{6,5},{7,4},{8,11},{9,10},{10,... | collective-permute-start | bytes 786440 | tf_op jit(solution)/shard_map/ppermute | solution.py:34
  6.3 26.1 %collective-permute-start.9 = (bf16[256,512]{1,0:T(8,128)(2,1)S(1)}, bf16[256,512]{1,0:T(8,128)(2,1)S(1)}, u32[]{:S(2)}, u32[]{:S(2)}) collective-permute-start(bf16[256,512]{1,0:T(8,128)(2,1)S(1)} %get-tuple-element.23), channel_id=1, source_target_pairs={{0,3},{1,2},{2,1},{3,0},{4,7},{5,6},{6,5},{7,4},{8,11},{9,10},{10,... | collective-permute-start | bytes 786440 | tf_op jit(solution)/shard_map/ppermute | solution.py:34
  6.4 37.1 %collective-permute-start.8 = (bf16[512,512]{1,0:T(8,128)(2,1)S(1)}, bf16[512,512]{1,0:T(8,128)(2,1)S(1)}, u32[]{:S(2)}, u32[]{:S(2)}) collective-permute-start(bf16[512,512]{1,0:T(8,128)(2,1)S(1)} %get-tuple-element.13.v_ref), channel_id=1, source_target_pairs={{0,1},{1,0},{2,3},{3,2},{4,5},{5,4},{6,7},{7,6},{8,9},{9,8},{10,11... | collective-permute-start | bytes 1572872 | tf_op jit(solution)/shard_map/ppermute | solution.py:34
  6.5 25.9 %collective-permute-start.2 = (bf16[256,512]{1,0:T(8,128)(2,1)}, bf16[256,512]{1,0:T(8,128)(2,1)S(1)}, u32[]{:S(2)}, u32[]{:S(2)}) collective-permute-start(bf16[256,512]{1,0:T(8,128)(2,1)} %get-tuple-element.22), channel_id=1, source_target_pairs={{0,3},{1,2},{2,1},{3,0},{4,7},{5,6},{6,5},{7,4},{8,11},{9,10},{10,... | collective-permute-start | bytes 786440 | tf_op jit(solution)/shard_map/ppermute | solution.py:34
  8.2 19.2 %collective-permute-start = (s32[1,4]{1,0:T(1,128)S(1)}, s32[1,4]{1,0:T(1,128)S(1)}, u32[]{:S(2)}, u32[]{:S(2)}) collective-permute-start(s32[1,4]{1,0:T(1,128)S(1)} %copy-done.16), channel_id=1, source_target_pairs={{0,64},{1,65},{2,66},{3,67},{4,68},{5,69},{6,70},{7,71},{8,72},{9,... | collective-permute-start | bytes 56 | tf_op jit(solution)/shard_map/ppermute | solution.py:34
  27.4 9.0 %collective-permute-start.1 = (bf16[256,512]{1,0:T(8,128)(2,1)S(1)}, bf16[256,512]{1,0:T(8,128)(2,1)}, u32[]{:S(2)}, u32[]{:S(2)}) collective-permute-start(bf16[256,512]{1,0:T(8,128)(2,1)S(1)} %get-tuple-element.24), channel_id=1, source_target_pairs={{0,3},{1,2},{2,1},{3,0},{4,7},{5,6},{6,5},{7,4},{8,11},{9,10},{10,... | collective-permute-start | bytes 786440 | tf_op jit(solution)/shard_map/ppermute | solution.py:34
  27.5 13.8 %collective-permute-start.12 = (bf16[256,512]{1,0:T(8,128)(2,1)S(1)}, bf16[256,512]{1,0:T(8,128)(2,1)S(1)}, u32[]{:S(2)}, u32[]{:S(2)}) collective-permute-start(bf16[256,512]{1,0:T(8,128)(2,1)S(1)} %collective-permute-done.10.vb), channel_id=1, source_target_pairs={{0,4},{1,61},{2,6},{3,63},{4,8},{5,1},{6,10},{7,3},{8,12},{9,5},{1... | collective-permute-start | bytes 786440 | tf_op jit(solution)/shard_map/ppermute | solution.py:34
  32.4 27.3 %collective-permute-start.7 = (bf16[512,512]{1,0:T(8,128)(2,1)S(1)}, bf16[512,512]{1,0:T(8,128)(2,1)S(1)}, u32[]{:S(2)}, u32[]{:S(2)}) collective-permute-start(bf16[512,512]{1,0:T(8,128)(2,1)S(1)} %copy-done), channel_id=1, source_target_pairs={{0,1},{1,0},{2,3},{3,2},{4,5},{5,4},{6,7},{7,6},{8,9},{9,8},{10,11... | collective-permute-start | bytes 1572872 | tf_op jit(solution)/shard_map/ppermute | solution.py:34
  32.4 10.3 %collective-permute-start.14 = (bf16[256,512]{1,0:T(8,128)(2,1)S(1)}, bf16[256,512]{1,0:T(8,128)(2,1)S(1)}, u32[]{:S(2)}, u32[]{:S(2)}) collective-permute-start(bf16[256,512]{1,0:T(8,128)(2,1)S(1)} %collective-permute-done.10.vb), channel_id=1, source_target_pairs={{0,67},{1,66},{2,65},{3,64},{4,71},{5,70},{6,69},{7,68},{8,75},{9,... | collective-permute-start | bytes 786440 | tf_op jit(solution)/shard_map/ppermute | solution.py:34
  33.3 0.7 %copy-start.3 = (bf16[256,512]{1,0:T(8,128)(2,1)}, bf16[256,512]{1,0:T(8,128)(2,1)S(1)}, u32[]{:S(2)}) copy-start(bf16[256,512]{1,0:T(8,128)(2,1)S(1)} %collective-permute-done.10.vb) | copy-start | bytes 786436
  36.4 8.4 %collective-permute-start.11 = (bf16[256,512]{1,0:T(8,128)(2,1)S(1)}, bf16[256,512]{1,0:T(8,128)(2,1)S(1)}, u32[]{:S(2)}, u32[]{:S(2)}) collective-permute-start(bf16[256,512]{1,0:T(8,128)(2,1)S(1)} %collective-permute-done.9.kb), channel_id=1, source_target_pairs={{0,4},{1,61},{2,6},{3,63},{4,8},{5,1},{6,10},{7,3},{8,12},{9,5},{1... | collective-permute-start | bytes 786440 | tf_op jit(solution)/shard_map/ppermute | solution.py:34
  41.3 0.7 %copy-start.7 = (bf16[256,512]{1,0:T(8,128)(2,1)}, bf16[256,512]{1,0:T(8,128)(2,1)S(1)}, u32[]{:S(2)}) copy-start(bf16[256,512]{1,0:T(8,128)(2,1)S(1)} %collective-permute-done.12.vd) | copy-start | bytes 786436
  42.0 13.0 %collective-permute-start.13 = (bf16[256,512]{1,0:T(8,128)(2,1)S(1)}, bf16[256,512]{1,0:T(8,128)(2,1)S(1)}, u32[]{:S(2)}, u32[]{:S(2)}) collective-permute-start(bf16[256,512]{1,0:T(8,128)(2,1)S(1)} %collective-permute-done.9.kb), channel_id=1, source_target_pairs={{0,67},{1,66},{2,65},{3,64},{4,71},{5,70},{6,69},{7,68},{8,75},{9,... | collective-permute-start | bytes 786440 | tf_op jit(solution)/shard_map/ppermute | solution.py:34
  42.0 0.7 %copy-start.5 = (bf16[256,512]{1,0:T(8,128)(2,1)}, bf16[256,512]{1,0:T(8,128)(2,1)S(1)}, u32[]{:S(2)}) copy-start(bf16[256,512]{1,0:T(8,128)(2,1)S(1)} %collective-permute-done.9.kb) | copy-start | bytes 786436
  42.7 0.7 %copy-start.9 = (bf16[256,512]{1,0:T(8,128)(2,1)}, bf16[256,512]{1,0:T(8,128)(2,1)S(1)}, u32[]{:S(2)}) copy-start(bf16[256,512]{1,0:T(8,128)(2,1)S(1)} %collective-permute-done.14.vc) | copy-start | bytes 786436
  43.4 19.1 %collective-permute-start.6 = (bf16[256,512]{1,0:T(8,128)(2,1)}, bf16[256,512]{1,0:T(8,128)(2,1)}, u32[]{:S(2)}, u32[]{:S(2)}) collective-permute-start(bf16[256,512]{1,0:T(8,128)(2,1)} %get-tuple-element.22), channel_id=1, source_target_pairs={{0,64},{1,65},{2,66},{3,67},{4,68},{5,69},{6,70},{7,71},{8,72},{9,... | collective-permute-start | bytes 786440 | tf_op jit(solution)/shard_map/ppermute | solution.py:34
  43.5 19.0 %collective-permute-start.4 = (bf16[256,512]{1,0:T(8,128)(2,1)S(1)}, bf16[256,512]{1,0:T(8,128)(2,1)}, u32[]{:S(2)}, u32[]{:S(2)}) collective-permute-start(bf16[256,512]{1,0:T(8,128)(2,1)S(1)} %collective-permute-done.2.vb), channel_id=1, source_target_pairs={{0,4},{1,61},{2,6},{3,63},{4,8},{5,1},{6,10},{7,3},{8,12},{9,5},{1... | collective-permute-start | bytes 786440 | tf_op jit(solution)/shard_map/ppermute | solution.py:34
  44.8 0.7 %copy-start.11 = (bf16[256,512]{1,0:T(8,128)(2,1)}, bf16[256,512]{1,0:T(8,128)(2,1)S(1)}, u32[]{:S(2)}) copy-start(bf16[256,512]{1,0:T(8,128)(2,1)S(1)} %collective-permute-done.11.kd) | copy-start | bytes 786436
  45.5 17.1 %collective-permute-start.3 = (bf16[256,512]{1,0:T(8,128)(2,1)}, bf16[256,512]{1,0:T(8,128)(2,1)}, u32[]{:S(2)}, u32[]{:S(2)}) collective-permute-start(bf16[256,512]{1,0:T(8,128)(2,1)} %collective-permute-done.1.kb), channel_id=1, source_target_pairs={{0,4},{1,61},{2,6},{3,63},{4,8},{5,1},{6,10},{7,3},{8,12},{9,5},{1... | collective-permute-start | bytes 786440 | tf_op jit(solution)/shard_map/ppermute | solution.py:34
  55.0 0.7 %copy-start.13 = (bf16[256,512]{1,0:T(8,128)(2,1)}, bf16[256,512]{1,0:T(8,128)(2,1)S(1)}, u32[]{:S(2)}) copy-start(bf16[256,512]{1,0:T(8,128)(2,1)S(1)} %collective-permute-done.13.kc) | copy-start | bytes 786436
  55.7 7.8 %collective-permute-start.5 = (bf16[256,512]{1,0:T(8,128)(2,1)}, bf16[256,512]{1,0:T(8,128)(2,1)}, u32[]{:S(2)}, u32[]{:S(2)}) collective-permute-start(bf16[256,512]{1,0:T(8,128)(2,1)} %collective-permute-done.1.kb), channel_id=1, source_target_pairs={{0,67},{1,66},{2,65},{3,64},{4,71},{5,70},{6,69},{7,68},{8,75},{9,... | collective-permute-start | bytes 786440 | tf_op jit(solution)/shard_map/ppermute | solution.py:34
  58.1 1.7 %copy-start.4 = (bf16[256,512]{1,0:T(8,128)(2,1)S(1)}, bf16[256,512]{1,0:T(8,128)(2,1)}, u32[]{:S(2)}) copy-start(bf16[256,512]{1,0:T(8,128)(2,1)} %copy-done.3) | copy-start | bytes 786436
  58.1 1.7 %copy-start.6 = (bf16[256,512]{1,0:T(8,128)(2,1)S(1)}, bf16[256,512]{1,0:T(8,128)(2,1)}, u32[]{:S(2)}) copy-start(bf16[256,512]{1,0:T(8,128)(2,1)} %copy-done.5) | copy-start | bytes 786436
  58.1 1.7 %copy-start.8 = (bf16[256,512]{1,0:T(8,128)(2,1)S(1)}, bf16[256,512]{1,0:T(8,128)(2,1)}, u32[]{:S(2)}) copy-start(bf16[256,512]{1,0:T(8,128)(2,1)} %copy-done.7) | copy-start | bytes 786436
  58.1 1.7 %copy-start.10 = (bf16[256,512]{1,0:T(8,128)(2,1)S(1)}, bf16[256,512]{1,0:T(8,128)(2,1)}, u32[]{:S(2)}) copy-start(bf16[256,512]{1,0:T(8,128)(2,1)} %copy-done.9) | copy-start | bytes 786436
  58.1 1.7 %copy-start.12 = (bf16[256,512]{1,0:T(8,128)(2,1)S(1)}, bf16[256,512]{1,0:T(8,128)(2,1)}, u32[]{:S(2)}) copy-start(bf16[256,512]{1,0:T(8,128)(2,1)} %copy-done.11) | copy-start | bytes 786436
  58.1 1.7 %copy-start.14 = (bf16[256,512]{1,0:T(8,128)(2,1)S(1)}, bf16[256,512]{1,0:T(8,128)(2,1)}, u32[]{:S(2)}) copy-start(bf16[256,512]{1,0:T(8,128)(2,1)} %copy-done.13) | copy-start | bytes 786436

commit v2 on v1

--- a/solution.py
+++ b/solution.py
@@ -1,3 +1,4 @@
+import functools
 import math
 
 import jax
@@ -13,6 +14,8 @@
 TILE = 128
 TILES = 4
 LISTED = 6
+BOUNDARY = 4
+EXTRA = 16
 PAIRS = 4
 BATCH = 4
 WIDTH = HEADS * HEAD_DIM
@@ -21,6 +24,7 @@
 LOWEST = -1e30
 
 VMEM = pl.BlockSpec(memory_space=pltpu.VMEM)
+ANY = pl.BlockSpec(memory_space=pl.ANY)
 SMEM = pl.BlockSpec(memory_space=pltpu.SMEM)
 
 
@@ -54,12 +58,46 @@
     return 1 - g, s
 
 
-def prepare_kernel(q_ref, v_ref, w_ref, v_out):
+def keys_kernel(keys, first, second, sems):
+    half = 2 * TILE
+    copies = [
+        pltpu.make_async_copy(keys.at[pl.ds(0, half)], first, sems.at[0]),
+        pltpu.make_async_copy(keys.at[pl.ds(half, half)], second, sems.at[1]),
+    ]
+    for copy in copies:
+        copy.start()
+    for copy in copies:
+        copy.wait()
+
+
+def split_keys(keys):
+    half = jax.ShapeDtypeStruct((2 * TILE, WIDTH), keys.dtype)
+    return pl.pallas_call(
+        keys_kernel,
+        out_shape=(half, half),
+        in_specs=[ANY],
+        out_specs=(VMEM, VMEM),
+        scratch_shapes=[pltpu.SemaphoreType.DMA((2,))],
+        compiler_params=pltpu.CompilerParams(vmem_limit_bytes=2 << 20),
+        cost_estimate=pl.CostEstimate(flops=400_000_000, bytes_accessed=8 << 20, transcendentals=0),
+        name="split_keys",
+    )(keys)
+
+
+def prepare_kernel(q_ref, v_ref, ids, v_first, v_second, v_all, w_ref):
+    lane = lax.broadcasted_iota(jnp.int32, (EXTRA, WIDTH), 1)
+    row = jnp.zeros((EXTRA, WIDTH), jnp.int32)
+    for j in range(BOUNDARY):
+        row = jnp.where(lane == j, ids[0, j], row)
+    v_first[2 * TILE :] = row.astype(jnp.float32).astype(jnp.bfloat16)
     for t in range(TILES):
         rows = pl.ds(t * TILE, TILE)
+        part = (v_first, v_second)[t // 2]
         for p in range(PAIRS):
             lanes = pl.ds(p * TILE, TILE)
-            v_out[rows, lanes] = v_ref[rows, lanes].T
+            vt = v_ref[rows, lanes].T
+            v_all[rows, lanes] = vt
+            part[pl.ds(t % 2 * TILE, TILE), lanes] = vt
             qt = q_ref[rows, lanes].T
             zero = jnp.zeros((HEAD_DIM, TILE), jnp.bfloat16)
             w_ref[t, p, :HEAD_DIM, :TILE] = qt[:HEAD_DIM]
@@ -68,19 +106,18 @@
             w_ref[t, p, HEAD_DIM:, TILE:] = qt[HEAD_DIM:]
 
 
-def prepare(q, v):
+def prepare(q, v, ids):
+    half = 2 * TILE
+    shapes = [(half + EXTRA, WIDTH), (half, WIDTH), v.shape, (TILES, PAIRS, TILE, 2 * TILE)]
     return pl.pallas_call(
         prepare_kernel,
-        out_shape=(
-            jax.ShapeDtypeStruct((TILES, PAIRS, TILE, 2 * TILE), jnp.bfloat16),
-            jax.ShapeDtypeStruct(v.shape, jnp.bfloat16),
-        ),
-        in_specs=[VMEM, VMEM],
-        out_specs=(VMEM, VMEM),
+        out_shape=[jax.ShapeDtypeStruct(shape, v.dtype) for shape in shapes],
+        in_specs=[VMEM, VMEM, SMEM],
+        out_specs=[VMEM] * 4,
         compiler_params=pltpu.CompilerParams(vmem_limit_bytes=8 << 20),
-        cost_estimate=pl.CostEstimate(flops=10**6, bytes_accessed=3 << 20, transcendentals=0),
+        cost_estimate=flops(1),
         name="prepare",
-    )(q, v)
+    )(q, v, ids)
 
 
 def list_items(lists_ref, live, source_of, items):
@@ -171,75 +208,92 @@
     )(lists, live, k, v, w)
 
 
-def pool_half(half, odd):
-    def source_of(ids_ref):
-        def find(pos):
-            other = jnp.where(odd, 2 * TILES, TILES)
-            beside = pos - other
-            is_beside = jnp.logical_and(beside >= 2 * half, beside < 2 * half + 2)
-            far = ids_ref[0, jnp.maximum(pos - 3 * TILES, 0)] - 2 * half
-            is_far = jnp.logical_and(pos >= 3 * TILES, jnp.logical_and(far >= 0, far < 2))
-            tile = jnp.where(is_beside, beside - 2 * half, jnp.where(is_far, far + 2, 0))
-            return jnp.logical_or(is_beside, is_far), tile
-
-        return find
-
-    return source_of
-
-
-def pick(inner, refs, k_all, v_all):
-    kb, vb, kd, vd, kc, vc = refs
-
-    @pl.when(inner)
-    def _():
-        k_all[: 2 * TILE] = kb[...]
-        v_all[: 2 * TILE] = vb[...]
-
-    @pl.when(jnp.logical_not(inner))
-    def _():
-        k_all[: 2 * TILE] = kd[...]
-        v_all[: 2 * TILE] = vd[...]
-
-    k_all[2 * TILE :] = kc[...]
-    v_all[2 * TILE :] = vc[...]
-
-
-def middle_kernel(lists, live, ids, slab, kn, vn, kb, vb, kd, vd, kc, vc, w_ref, acc0, peak0, total0, acc, peak, total, items, k_all, v_all):
-    odd = lax.rem(slab[0], 2) == 1
-    inner = jnp.logical_or(lax.rem(slab[0], 4) == 1, lax.rem(slab[0], 4) == 2)
-
-    def near(pos):
-        at = pos - jnp.where(odd, TILES, 2 * TILES)
+def is_inner():
+    at = lax.rem(lax.axis_index("slab"), 4)
+    return jnp.logical_or(at == 1, at == 2)
+
+
+def is_odd():
+    return lax.rem(lax.axis_index("slab"), 2) == 1
+
+
+def find_near():
+    base = jnp.where(is_odd(), TILES, 2 * TILES)
+
+    def find(pos):
+        at = pos - base
         here = jnp.logical_and(at >= 0, at < TILES)
         return here, jnp.where(here, at, 0)
 
-    batches = list_items(lists, live[0], near, items)
-    attend_items(batches, items, kn, vn, w_ref, acc, peak, total)
-    pick(inner, (kb, vb, kd, vd, kc, vc), k_all, v_all)
-    batches = list_items(lists, live[0], pool_half(0, odd)(ids), items)
-    attend_items(batches, items, k_all, v_all, w_ref, acc, peak, total)
-
-
-def middle_stage(lists, live, ids, slab, tiles, w, state):
-    return pl.pallas_call(
-        middle_kernel,
+    return find
+
+
+def find_other(half):
+    base = jnp.where(is_odd(), 2 * TILES, TILES) + 2 * half
+
+    def find(pos):
+        at = pos - base
+        here = jnp.logical_and(at >= 0, at < 2)
+        return here, jnp.where(here, at, 0)
+
+    return find
+
+
+def find_far(marks, half):
+    lane = lax.broadcasted_iota(jnp.int32, (1, TILE), 1)
+    line = marks[2 * TILE : 2 * TILE + EXTRA, :TILE].astype(jnp.float32)[:1]
+    ids = [jnp.sum(jnp.where(lane == j, line, 0.0)).astype(jnp.int32) for j in range(BOUNDARY)]
+
+    def find(pos):
+        at = jnp.int32(-1)
+        for j in range(BOUNDARY):
+            at = jnp.where(pos == 3 * TILES + j, ids[j] - 2 * half, at)
+        here = jnp.logical_and(at >= 0, at < 2)
+        return here, jnp.where(here, at, 0)
+
+    return find
+
+
+def near_kernel(lists, live, k_ref, v_ref, w_ref, acc0, peak0, total0, acc, peak, total, items):
+    batches = list_items(lists, live[0], find_near(), items)
+    attend_items(batches, items, k_ref, v_ref, w_ref, acc, peak, total)
+
+
+def other_kernel(half, lists, live, kb, vb, kd, vd, w_ref, acc0, peak0, total0, acc, peak, total, items):
+    batches = list_items(lists, live[0], find_other(half), items)
+
+    @pl.when(is_inner())
+    def _():
+        attend_items(batches, items, kb, vb, w_ref, acc, peak, total)
+
+    @pl.when(jnp.logical_not(is_inner()))
+    def _():
+        attend_items(batches, items, kd, vd, w_ref, acc, peak, total)
+
+
+def far_kernel(lists, live, k_ref, v_ref, w_ref, acc0, peak0, total0, acc, peak, total, items):
+    batches = list_items(lists, live[0], find_far(v_ref, 0), items)
+    attend_items(batches, items, k_ref, v_ref, w_ref, acc, peak, total)
+
+
+def stage(kernel, lists, live, tiles, w, state):
+    args = (lists, live, *tiles, w, *state)
+    first = len(args) - 3
+    return pl.pallas_call(
+        kernel,
         out_shape=STATE,
-        in_specs=[SMEM] * 4 + [VMEM] * 12,
+        in_specs=[SMEM] * 2 + [VMEM] * (len(args) - 2),
         out_specs=(VMEM,) * 3,
-        input_output_aliases={13: 0, 14: 1, 15: 2},
-        scratch_shapes=[ITEMS, pltpu.VMEM((4 * TILE, WIDTH), jnp.bfloat16), pltpu.VMEM((4 * TILE, WIDTH), jnp.bfloat16)],
-        compiler_params=pltpu.CompilerParams(vmem_limit_bytes=20 << 20),
-        cost_estimate=flops(16),
-        name="middle_stage",
-    )(lists, live, ids, slab, *tiles, w, *state)
-
-
-def last_kernel(lists, live, ids, slab, kb, vb, kd, vd, kc, vc, w_ref, acc, peak, total, out, items, k_all, v_all):
-    odd = lax.rem(slab[0], 2) == 1
-    inner = jnp.logical_or(lax.rem(slab[0], 4) == 1, lax.rem(slab[0], 4) == 2)
-    pick(inner, (kb, vb, kd, vd, kc, vc), k_all, v_all)
-    batches = list_items(lists, live[0], pool_half(1, odd)(ids), items)
-    attend_items(batches, items, k_all, v_all, w_ref, acc, peak, total)
+        input_output_aliases={first: 0, first + 1: 1, first + 2: 2},
+        scratch_shapes=[ITEMS],
+        compiler_params=pltpu.CompilerParams(vmem_limit_bytes=12 << 20),
+        cost_estimate=flops(8),
+    )(*args)
+
+
+def last_kernel(lists, live, marks, k_ref, v_ref, w_ref, acc, peak, total, out, items):
+    batches = list_items(lists, live[0], find_far(marks, 1), items)
+    attend_items(batches, items, k_ref, v_ref, w_ref, acc, peak, total)
     for t in range(TILES):
         rows = pl.ds(t * TILE, TILE)
 
@@ -259,36 +313,36 @@
             out[rows] = jnp.zeros((TILE, WIDTH), jnp.bfloat16)
 
 
-def last_stage(lists, live, ids, slab, tiles, w, state):
+def last_stage(lists, live, tiles, w, state):
     return pl.pallas_call(
         last_kernel,
         out_shape=jax.ShapeDtypeStruct((TILES * TILE, WIDTH), jnp.bfloat16),
-        in_specs=[SMEM] * 4 + [VMEM] * 10,
+        in_specs=[SMEM] * 2 + [VMEM] * 7,
         out_specs=VMEM,
-        scratch_shapes=[ITEMS, pltpu.VMEM((4 * TILE, WIDTH), jnp.bfloat16), pltpu.VMEM((4 * TILE, WIDTH), jnp.bfloat16)],
-        compiler_params=pltpu.CompilerParams(vmem_limit_bytes=20 << 20),
+        scratch_shapes=[ITEMS],
+        compiler_params=pltpu.CompilerParams(vmem_limit_bytes=12 << 20),
         cost_estimate=flops(8),
         name="last_stage",
-    )(lists, live, ids, slab, *tiles, w, *state)
+    )(lists, live, *tiles, w, *state)
 
 
 def shards(queries, keys, values, neighbours, live_tiles, boundary_ids):
-    half = 2 * TILE
-    slab = lax.axis_index("slab").astype(jnp.int32)[None]
-    ka, kz = keys[:half], keys[half:]
-    w, vt = prepare(queries, values)
-    va, vz = vt[:half], vt[half:]
+    ka, kz = split_keys(keys)
+    va, vz, vt, w = prepare(queries, values, boundary_ids)
     near = move(keys, to_chip), move(vt, to_chip)
     cross = [move(x, to_cross) for x in (ka, va, kz, vz)]
     far_last = move(vz, to_group)
-    ids = move(boundary_ids, to_group)
     far = [move(cross[i], to_forward) for i in range(3)] + [far_last]
     along = [move(cross[i], to_along) for i in range(4)]
+    common = neighbours, live_tiles
     state = first_stage(neighbours, live_tiles, keys, vt, w)
-    tiles = (*near, cross[0], cross[1], along[0], along[1], far[0], far[1])
-    state = middle_stage(neighbours, live_tiles, ids, slab, tiles, w, state)
-    tiles = (cross[2], cross[3], along[2], along[3], far[2], far[3])
-    return last_stage(neighbours, live_tiles, ids, slab, tiles, w, state)
+    state = stage(near_kernel, *common, near, w, state)
+    tiles = cross[0], cross[1], along[0], along[1]
+    state = stage(functools.partial(other_kernel, 0), *common, tiles, w, state)
+    state = stage(far_kernel, *common, (far[0], far[1]), w, state)
+    tiles = cross[2], cross[3], along[2], along[3]
+    state = stage(functools.partial(other_kernel, 1), *common, tiles, w, state)
+    return last_stage(neighbours, live_tiles, (far[1], far[2], far[3]), w, state)
 
 
 def solution(mesh):

time: 68.1 us -> 59 us (0.87); the launches traced: 67 us -> 58.6 us
  local copies, waits for them, and re-layouts: 7.18 us -> 1.8 us
  starting transfers between devices: 27 us -> 23.9 us
  Pallas kernels: 8.15 us -> 11.1 us
  waiting for transfers between devices: 23.8 us -> 21 us
    unnamed x34 -> x12, local copies, waits for them, and re-layouts: 6.41 us -> 1.8 us
    pallas_call x2 -> x6, Pallas kernels: 3.11 us -> 6.63 us  [the longest x4 5.67 us: stage(): pl.pallas_call(kernel, out_shape=STATE, in_specs=[SMEM] * 2 + [VMEM] * (l...]
    ppermute x15 -> x14, starting transfers between devices: 27 us -> 23.9 us  [move(): return lax.ppermute(block, AXES, route)]
    ppermute x15 -> x14, waiting for transfers between devices: 23.8 us -> 21 us  [move(): return lax.ppermute(block, AXES, route)]
    slice x2 -> x0, local copies, waits for them, and re-layouts: 0.77 us -> none  [the longest x1 0.74 us: shards(): va, vz = (vt[:half], vt[half:])]
  transfers between devices with their start and end apart: 15 -> 14, of which waited for: 4 -> 5; matrix products, arithmetic and copies ran while one was open for 0% -> 0% of each run, Pallas kernels for 6% -> 14%
where the time goes in v2:
time: 59 us; the launch traced here: 58.6 us
  starting transfers between devices  23.9 us (41%)
  waiting for transfers between devices  21 us (36%)
  Pallas kernels  11.1 us (19%)
  local copies, waits for them, and re-layouts  1.8 us (3%)
  between operations  0.75 us (1%)
    ppermute x14, starting transfers between devices, move(): return lax.ppermute(block, AXES, route)  23.9 us
    ppermute x14, waiting for transfers between devices, move(): return lax.ppermute(block, AXES, route)  21 us
    pallas_call x4, Pallas kernels, stage(): pl.pallas_call(kernel, out_shape=STATE, in_specs=[SMEM] * 2 + [VMEM] * (l...  5.67 us
    pallas_call x1, Pallas kernels, last_stage(): pl.pallas_call(last_kernel, out_shape=jax.ShapeDtypeStruct((TILES * TILE,...  2.85 us
    unnamed x12, local copies, waits for them, and re-layouts  1.8 us
    pallas_call x1, Pallas kernels, first_stage(): pl.pallas_call(first_kernel, out_shape=STATE, in_specs=[SMEM, SMEM] + [VM...  1.58 us
  transfers between devices with their start and end apart: 14, of which 5 were waited for; matrix products, arithmetic and copies ran while one was open for 0% of the time, Pallas kernels for 14%

profile of v2, /device:TPU:1, one launch (start us, length us, event | category | flops | bytes accessed | tf_op | source)
XLA Modules:
  0.0 58.6 jit_solution(6216001424908726993)
XLA Ops:
  0.0 0.0 copy-start
  0.0 0.0 copy-start.1
  0.0 0.0 copy-start.2
  0.0 1.1 %copy-done.2 = bf16[512,512]{1,0:T(8,128)(2,1)S(1)} copy-done((bf16[512,512]{1,0:T(8,128)(2,1)S(1)}, bf16[512,512]{1,0:T(8,128)(2,1)}, u32[]{:S(2)}) %copy-start.2) | copy-done | bytes 524312
  1.1 0.0 copy-start.3
  1.1 0.0 copy-start.4
  1.1 0.1 split_keys.1
  1.2 3.1 %collective-permute-start.8 = (bf16[256,512]{1,0:T(8,128)(2,1)S(1)}, bf16[256,512]{1,0:T(8,128)(2,1)S(1)}, u32[]{:S(2)}, u32[]{:S(2)}) collective-permute-start(bf16[256,512]{1,0:T(8,128)(2,1)S(1)} %get-tuple-element.30), channel_id=1, source_target_pairs={{0,3},{1,2},{2,1},{3,0},{4,7},{5,6},{6,5},{7,4},{8,11},{9,10},{10,... | collective-permute-start | bytes 786440 | tf_op jit(solution)/shard_map/ppermute | solution.py:38
  4.3 0.0 copy-done
  4.3 0.0 copy-done.1
  4.3 0.0 copy-start.5
  4.3 0.7 %copy-done.5 = s32[1,4]{1,0:T(1,128)S(1)} copy-done((s32[1,4]{1,0:T(1,128)S(1)}, s32[1,4]{1,0:T(1,128)}, u32[]{:S(2)}) %copy-start.5) | copy-done | bytes 40
  5.0 0.9 %prepare.1 = (bf16[272,512]{1,0:T(8,128)(2,1)S(1)}, bf16[256,512]{1,0:T(8,128)(2,1)S(1)}, bf16[512,512]{1,0:T(8,128)(2,1)S(1)}, bf16[4,4,128,256]{3,2,1,0:T(8,128)(2,1)S(1)}) custom-call(bf16[512,512]{1,0:T(8,128)(2,1)S(1)} %copy-done, bf16[512,512]{1,0:T(8,128)(2,1)S(1)} %copy-done.1, s32[1,4]{1,0:T(1,128)S(1)} %copy-done.5), custom_call_target="tpu_custom_call" | custom-call | flops 40000000 | bytes 1048576 | tf_op jit(solution)/shard_map/prepare/pallas_call | solution.py:112
  5.9 0.1 collective-permute-start.13
  6.0 0.1 collective-permute-start
  6.1 0.0 copy-done.3
  6.1 0.4 collective-permute-start.12
  6.5 1.7 %collective-permute-start.5 = (bf16[256,512]{1,0:T(8,128)(2,1)S(1)}, bf16[256,512]{1,0:T(8,128)(2,1)S(1)}, u32[]{:S(2)}, u32[]{:S(2)}) collective-permute-start(bf16[256,512]{1,0:T(8,128)(2,1)S(1)} %get-tuple-element.28), channel_id=1, source_target_pairs={{0,3},{1,2},{2,1},{3,0},{4,7},{5,6},{6,5},{7,4},{8,11},{9,10},{10,... | collective-permute-start | bytes 786440 | tf_op jit(solution)/shard_map/ppermute | solution.py:38
  8.2 3.2 %collective-permute-done.8.kb = bf16[256,512]{1,0:T(8,128)(2,1)S(1)} collective-permute-done((bf16[256,512]{1,0:T(8,128)(2,1)S(1)}, bf16[256,512]{1,0:T(8,128)(2,1)S(1)}, u32[]{:S(2)}, u32[]{:S(2)}) %collective-permute-start.8) | collective-permute-done | bytes 262176 | tf_op jit(solution)/shard_map/ppermute | solution.py:38
  11.5 1.4 %collective-permute-start.2 = (bf16[256,512]{1,0:T(8,128)(2,1)S(1)}, bf16[256,512]{1,0:T(8,128)(2,1)S(1)}, u32[]{:S(2)}, u32[]{:S(2)}) collective-permute-start(bf16[256,512]{1,0:T(8,128)(2,1)S(1)} %get-tuple-element.27), channel_id=1, source_target_pairs={{0,3},{1,2},{2,1},{3,0},{4,7},{5,6},{6,5},{7,4},{8,11},{9,10},{10,... | collective-permute-start | bytes 786440 | tf_op jit(solution)/shard_map/ppermute | solution.py:38
  12.9 10.2 %collective-permute-done.5.vb = bf16[256,512]{1,0:T(8,128)(2,1)S(1)} collective-permute-done((bf16[256,512]{1,0:T(8,128)(2,1)S(1)}, bf16[256,512]{1,0:T(8,128)(2,1)S(1)}, u32[]{:S(2)}, u32[]{:S(2)}) %collective-permute-start.5) | collective-permute-done | bytes 262176 | tf_op jit(solution)/shard_map/ppermute | solution.py:38
  23.0 4.9 %collective-permute-start.10 = (bf16[256,512]{1,0:T(8,128)(2,1)S(1)}, bf16[256,512]{1,0:T(8,128)(2,1)S(1)}, u32[]{:S(2)}, u32[]{:S(2)}) collective-permute-start(bf16[256,512]{1,0:T(8,128)(2,1)S(1)} %collective-permute-done.8.kb), channel_id=1, source_target_pairs={{0,4},{1,61},{2,6},{3,63},{4,8},{5,1},{6,10},{7,3},{8,12},{9,5},{1... | collective-permute-start | bytes 786440 | tf_op jit(solution)/shard_map/ppermute | solution.py:38
  28.0 0.0 collective-permute-done.vb
  28.0 0.5 collective-permute-start.11
  28.5 0.0 collective-permute-done.2.kb
  28.5 3.7 %collective-permute-start.9 = (bf16[256,512]{1,0:T(8,128)(2,1)S(1)}, bf16[256,512]{1,0:T(8,128)(2,1)S(1)}, u32[]{:S(2)}, u32[]{:S(2)}) collective-permute-start(bf16[256,512]{1,0:T(8,128)(2,1)S(1)} %collective-permute-done.8.kb), channel_id=1, source_target_pairs={{0,67},{1,66},{2,65},{3,64},{4,71},{5,70},{6,69},{7,68},{8,75},{9,... | collective-permute-start | bytes 786440 | tf_op jit(solution)/shard_map/ppermute | solution.py:38
  32.2 0.0 collective-permute-done.13.v_ref
  32.2 0.0 collective-permute-start.1
  32.2 0.0 collective-permute-done.12.k_ref
  32.2 5.0 %collective-permute-start.7 = (bf16[256,512]{1,0:T(8,128)(2,1)S(1)}, bf16[256,512]{1,0:T(8,128)(2,1)S(1)}, u32[]{:S(2)}, u32[]{:S(2)}) collective-permute-start(bf16[256,512]{1,0:T(8,128)(2,1)S(1)} %collective-permute-done.5.vb), channel_id=1, source_target_pairs={{0,4},{1,61},{2,6},{3,63},{4,8},{5,1},{6,10},{7,3},{8,12},{9,5},{1... | collective-permute-start | bytes 786440 | tf_op jit(solution)/shard_map/ppermute | solution.py:38
  37.2 0.0 collective-permute-done.10.kd
  37.2 0.5 collective-permute-start.6
  37.8 1.6 %collective-permute-done.9.k_ref = bf16[256,512]{1,0:T(8,128)(2,1)S(1)} collective-permute-done((bf16[256,512]{1,0:T(8,128)(2,1)S(1)}, bf16[256,512]{1,0:T(8,128)(2,1)S(1)}, u32[]{:S(2)}, u32[]{:S(2)}) %collective-permute-start.9) | collective-permute-done | bytes 262176 | tf_op jit(solution)/shard_map/ppermute | solution.py:38
  39.4 1.4 %collective-permute-start.4 = (bf16[256,512]{1,0:T(8,128)(2,1)S(1)}, bf16[256,512]{1,0:T(8,128)(2,1)S(1)}, u32[]{:S(2)}, u32[]{:S(2)}) collective-permute-start(bf16[256,512]{1,0:T(8,128)(2,1)S(1)} %get-tuple-element.28), channel_id=1, source_target_pairs={{0,64},{1,65},{2,66},{3,67},{4,68},{5,69},{6,70},{7,71},{8,72},{9,... | collective-permute-start | bytes 786440 | tf_op jit(solution)/shard_map/ppermute | solution.py:38
  40.7 0.0 collective-permute-done.11.vd
  40.7 1.0 %collective-permute-start.3 = (bf16[256,512]{1,0:T(8,128)(2,1)S(1)}, bf16[256,512]{1,0:T(8,128)(2,1)S(1)}, u32[]{:S(2)}, u32[]{:S(2)}) collective-permute-start(bf16[256,512]{1,0:T(8,128)(2,1)S(1)} %collective-permute-done.2.kb), channel_id=1, source_target_pairs={{0,67},{1,66},{2,65},{3,64},{4,71},{5,70},{6,69},{7,68},{8,75},{9,... | collective-permute-start | bytes 786440 | tf_op jit(solution)/shard_map/ppermute | solution.py:38
  42.4 0.0 copy-done.4
  42.4 1.6 %first_stage.1 = (f32[5,512,128]{2,1,0:T(8,128)S(1)}, f32[5,8,128]{2,1,0:T(8,128)S(1)}, f32[5,8,128]{2,1,0:T(8,128)S(1)}) custom-call(s32[4,6]{1,0:T(4,128)S(1)} %copy-done.4, s32[1]{0:T(128)S(6)} %copy.31.live, bf16[512,512]{1,0:T(8,128)(2,1)S(1)} %copy-done.3, bf16[512,512]{1,0:T(8,128)(2,1)S(1)} %get-tuple-element.31.v_ref, ...), custom_call_target="tpu_custom_call" | custom-call | flops 320000000 | bytes 1048576 | tf_op jit(solution)/shard_map/first_stage/pallas_call | solution.py:199
  44.0 1.6 %shard_map.64 = (f32[5,512,128]{2,1,0:T(8,128)S(1)}, f32[5,8,128]{2,1,0:T(8,128)S(1)}, f32[5,8,128]{2,1,0:T(8,128)S(1)}) custom-call(s32[4,6]{1,0:T(4,128)S(1)} %copy-done.4, s32[1]{0:T(128)S(6)} %copy.31.live, bf16[512,512]{1,0:T(8,128)(2,1)S(1)} %collective-permute-done.12.k_ref, ...), custom_call_target="tpu_custom_call", output_to_operand_aliasing={{0}: (5, {}), {1}: (6, {}), {2}: (7, {})} | custom-call | flops 320000000 | bytes 1048576 | tf_op jit(solution)/shard_map/pallas_call | solution.py:282
  45.6 1.6 %shard_map.65 = (f32[5,512,128]{2,1,0:T(8,128)S(1)}, f32[5,8,128]{2,1,0:T(8,128)S(1)}, f32[5,8,128]{2,1,0:T(8,128)S(1)}) custom-call(s32[4,6]{1,0:T(4,128)S(1)} %copy-done.4, s32[1]{0:T(128)S(6)} %copy.31.live, bf16[256,512]{1,0:T(8,128)(2,1)S(1)} %collective-permute-done.8.kb, ...), custom_call_target="tpu_custom_call", output_to_operand_aliasing={{0}: (7, {}), {1}: (8, {}), {2}: (9, {})} | custom-call | flops 320000000 | bytes 1048576 | tf_op jit(solution)/shard_map/pallas_call | solution.py:282
  47.2 3.8 %collective-permute-done.1.v_ref.marks = bf16[272,512]{1,0:T(8,128)(2,1)S(1)} collective-permute-done((bf16[272,512]{1,0:T(8,128)(2,1)S(1)}, bf16[272,512]{1,0:T(8,128)(2,1)S(1)}, u32[]{:S(2)}, u32[]{:S(2)}) %collective-permute-start.1) | collective-permute-done | bytes 278560 | tf_op jit(solution)/shard_map/ppermute | solution.py:38
  51.0 0.9 %shard_map.66 = (f32[5,512,128]{2,1,0:T(8,128)S(1)}, f32[5,8,128]{2,1,0:T(8,128)S(1)}, f32[5,8,128]{2,1,0:T(8,128)S(1)}) custom-call(s32[4,6]{1,0:T(4,128)S(1)} %copy-done.4, s32[1]{0:T(128)S(6)} %copy.31.live, bf16[256,512]{1,0:T(8,128)(2,1)S(1)} %collective-permute-done.9.k_ref, ...), custom_call_target="tpu_custom_call", output_to_operand_aliasing={{0}: (5, {}), {1}: (6, {}), {2}: (7, {})} | custom-call | flops 320000000 | bytes 1048576 | tf_op jit(solution)/shard_map/pallas_call | solution.py:282
  51.8 0.0 collective-permute-done.7.vd
  51.9 0.0 collective-permute-done.6.kd
  51.9 1.6 %shard_map.67 = (f32[5,512,128]{2,1,0:T(8,128)S(1)}, f32[5,8,128]{2,1,0:T(8,128)S(1)}, f32[5,8,128]{2,1,0:T(8,128)S(1)}) custom-call(s32[4,6]{1,0:T(4,128)S(1)} %copy-done.4, s32[1]{0:T(128)S(6)} %copy.31.live, bf16[256,512]{1,0:T(8,128)(2,1)S(1)} %collective-permute-done.2.kb, ...), custom_call_target="tpu_custom_call", output_to_operand_aliasing={{0}: (7, {}), {1}: (8, {}), {2}: (9, {})} | custom-call | flops 320000000 | bytes 1048576 | tf_op jit(solution)/shard_map/pallas_call | solution.py:282
  53.5 0.0 collective-permute-done.4.v_ref
  53.5 2.2 %collective-permute-done.3.k_ref = bf16[256,512]{1,0:T(8,128)(2,1)S(1)} collective-permute-done((bf16[256,512]{1,0:T(8,128)(2,1)S(1)}, bf16[256,512]{1,0:T(8,128)(2,1)S(1)}, u32[]{:S(2)}, u32[]{:S(2)}) %collective-permute-start.3) | collective-permute-done | bytes 262176 | tf_op jit(solution)/shard_map/ppermute | solution.py:38
  55.7 2.8 %last_stage.1 = bf16[512,512]{1,0:T(8,128)(2,1)} custom-call(s32[4,6]{1,0:T(4,128)S(1)} %copy-done.4, s32[1]{0:T(128)S(6)} %copy.31.live, bf16[272,512]{1,0:T(8,128)(2,1)S(1)} %collective-permute-done.1.v_ref.marks, bf16[256,512]{1,0:T(8,128)(2,1)S(1)} %collective-permute-done.3.k_ref, bf16[256,512]{1,0:T(8,128)(2,1)S(1)} %collective-permute-done.4.v_ref, ...), custom_call_target="tpu_custom_call" | custom-call | flops 320000000 | bytes 1048576 | tf_op jit(solution)/shard_map/last_stage/pallas_call | solution.py:317
Async XLA Ops:
  0.0 4.3 %copy-start = (bf16[512,512]{1,0:T(8,128)(2,1)S(1)}, bf16[512,512]{1,0:T(8,128)(2,1)}, u32[]{:S(2)}) copy-start(bf16[512,512]{1,0:T(8,128)(2,1)} %q_ref.1) | copy-start | bytes 1572868
  0.0 4.3 %copy-start.1 = (bf16[512,512]{1,0:T(8,128)(2,1)S(1)}, bf16[512,512]{1,0:T(8,128)(2,1)}, u32[]{:S(2)}) copy-start(bf16[512,512]{1,0:T(8,128)(2,1)} %v_ref.1) | copy-start | bytes 1572868
  0.0 1.1 %copy-start.2 = (bf16[512,512]{1,0:T(8,128)(2,1)S(1)}, bf16[512,512]{1,0:T(8,128)(2,1)}, u32[]{:S(2)}) copy-start(bf16[512,512]{1,0:T(8,128)(2,1)} %k_ref.1) | copy-start | bytes 1572868
  1.1 5.0 %copy-start.3 = (bf16[512,512]{1,0:T(8,128)(2,1)S(1)}, bf16[512,512]{1,0:T(8,128)(2,1)}, u32[]{:S(2)}) copy-start(bf16[512,512]{1,0:T(8,128)(2,1)} %k_ref.1) | copy-start | bytes 1572868
  1.1 41.3 %copy-start.4 = (s32[4,6]{1,0:T(4,128)S(1)}, s32[4,6]{1,0:T(4,128)}, u32[]{:S(2)}) copy-start(s32[4,6]{1,0:T(4,128)} %lists.11) | copy-start | bytes 292
  1.2 10.3 %collective-permute-start.8 = (bf16[256,512]{1,0:T(8,128)(2,1)S(1)}, bf16[256,512]{1,0:T(8,128)(2,1)S(1)}, u32[]{:S(2)}, u32[]{:S(2)}) collective-permute-start(bf16[256,512]{1,0:T(8,128)(2,1)S(1)} %get-tuple-element.30), channel_id=1, source_target_pairs={{0,3},{1,2},{2,1},{3,0},{4,7},{5,6},{6,5},{7,4},{8,11},{9,10},{10,... | collective-permute-start | bytes 786440 | tf_op jit(solution)/shard_map/ppermute | solution.py:38
  4.3 0.7 %copy-start.5 = (s32[1,4]{1,0:T(1,128)S(1)}, s32[1,4]{1,0:T(1,128)}, u32[]{:S(2)}) copy-start(s32[1,4]{1,0:T(1,128)} %ids.1) | copy-start | bytes 52
  5.9 26.3 %collective-permute-start.13 = (bf16[512,512]{1,0:T(8,128)(2,1)S(1)}, bf16[512,512]{1,0:T(8,128)(2,1)S(1)}, u32[]{:S(2)}, u32[]{:S(2)}) collective-permute-start(bf16[512,512]{1,0:T(8,128)(2,1)S(1)} %get-tuple-element.31.v_ref), channel_id=1, source_target_pairs={{0,1},{1,0},{2,3},{3,2},{4,5},{5,4},{6,7},{7,6},{8,9},{9,8},{10,11... | collective-permute-start | bytes 1572872 | tf_op jit(solution)/shard_map/ppermute | solution.py:38
  6.0 22.0 %collective-permute-start = (bf16[272,512]{1,0:T(8,128)(2,1)S(1)}, bf16[272,512]{1,0:T(8,128)(2,1)S(1)}, u32[]{:S(2)}, u32[]{:S(2)}) collective-permute-start(bf16[272,512]{1,0:T(8,128)(2,1)S(1)} %get-tuple-element.26), channel_id=1, source_target_pairs={{0,3},{1,2},{2,1},{3,0},{4,7},{5,6},{6,5},{7,4},{8,11},{9,10},{10,... | collective-permute-start | bytes 835592 | tf_op jit(solution)/shard_map/ppermute | solution.py:38
  6.1 26.1 %collective-permute-start.12 = (bf16[512,512]{1,0:T(8,128)(2,1)S(1)}, bf16[512,512]{1,0:T(8,128)(2,1)S(1)}, u32[]{:S(2)}, u32[]{:S(2)}) collective-permute-start(bf16[512,512]{1,0:T(8,128)(2,1)S(1)} %copy-done.3), channel_id=1, source_target_pairs={{0,1},{1,0},{2,3},{3,2},{4,5},{5,4},{6,7},{7,6},{8,9},{9,8},{10,11... | collective-permute-start | bytes 1572872 | tf_op jit(solution)/shard_map/ppermute | solution.py:38
  6.5 16.5 %collective-permute-start.5 = (bf16[256,512]{1,0:T(8,128)(2,1)S(1)}, bf16[256,512]{1,0:T(8,128)(2,1)S(1)}, u32[]{:S(2)}, u32[]{:S(2)}) collective-permute-start(bf16[256,512]{1,0:T(8,128)(2,1)S(1)} %get-tuple-element.28), channel_id=1, source_target_pairs={{0,3},{1,2},{2,1},{3,0},{4,7},{5,6},{6,5},{7,4},{8,11},{9,10},{10,... | collective-permute-start | bytes 786440 | tf_op jit(solution)/shard_map/ppermute | solution.py:38
  11.5 17.1 %collective-permute-start.2 = (bf16[256,512]{1,0:T(8,128)(2,1)S(1)}, bf16[256,512]{1,0:T(8,128)(2,1)S(1)}, u32[]{:S(2)}, u32[]{:S(2)}) collective-permute-start(bf16[256,512]{1,0:T(8,128)(2,1)S(1)} %get-tuple-element.27), channel_id=1, source_target_pairs={{0,3},{1,2},{2,1},{3,0},{4,7},{5,6},{6,5},{7,4},{8,11},{9,10},{10,... | collective-permute-start | bytes 786440 | tf_op jit(solution)/shard_map/ppermute | solution.py:38
  23.0 14.2 %collective-permute-start.10 = (bf16[256,512]{1,0:T(8,128)(2,1)S(1)}, bf16[256,512]{1,0:T(8,128)(2,1)S(1)}, u32[]{:S(2)}, u32[]{:S(2)}) collective-permute-start(bf16[256,512]{1,0:T(8,128)(2,1)S(1)} %collective-permute-done.8.kb), channel_id=1, source_target_pairs={{0,4},{1,61},{2,6},{3,63},{4,8},{5,1},{6,10},{7,3},{8,12},{9,5},{1... | collective-permute-start | bytes 786440 | tf_op jit(solution)/shard_map/ppermute | solution.py:38
  28.0 12.8 %collective-permute-start.11 = (bf16[272,512]{1,0:T(8,128)(2,1)S(1)}, bf16[272,512]{1,0:T(8,128)(2,1)S(1)}, u32[]{:S(2)}, u32[]{:S(2)}) collective-permute-start(bf16[272,512]{1,0:T(8,128)(2,1)S(1)} %collective-permute-done.vb), channel_id=1, source_target_pairs={{0,4},{1,61},{2,6},{3,63},{4,8},{5,1},{6,10},{7,3},{8,12},{9,5},{1... | collective-permute-start | bytes 835592 | tf_op jit(solution)/shard_map/ppermute | solution.py:38
  28.5 10.8 %collective-permute-start.9 = (bf16[256,512]{1,0:T(8,128)(2,1)S(1)}, bf16[256,512]{1,0:T(8,128)(2,1)S(1)}, u32[]{:S(2)}, u32[]{:S(2)}) collective-permute-start(bf16[256,512]{1,0:T(8,128)(2,1)S(1)} %collective-permute-done.8.kb), channel_id=1, source_target_pairs={{0,67},{1,66},{2,65},{3,64},{4,71},{5,70},{6,69},{7,68},{8,75},{9,... | collective-permute-start | bytes 786440 | tf_op jit(solution)/shard_map/ppermute | solution.py:38
  32.2 18.7 %collective-permute-start.1 = (bf16[272,512]{1,0:T(8,128)(2,1)S(1)}, bf16[272,512]{1,0:T(8,128)(2,1)S(1)}, u32[]{:S(2)}, u32[]{:S(2)}) collective-permute-start(bf16[272,512]{1,0:T(8,128)(2,1)S(1)} %collective-permute-done.vb), channel_id=1, source_target_pairs={{0,67},{1,66},{2,65},{3,64},{4,71},{5,70},{6,69},{7,68},{8,75},{9,... | collective-permute-start | bytes 835592 | tf_op jit(solution)/shard_map/ppermute | solution.py:38
  32.2 19.6 %collective-permute-start.7 = (bf16[256,512]{1,0:T(8,128)(2,1)S(1)}, bf16[256,512]{1,0:T(8,128)(2,1)S(1)}, u32[]{:S(2)}, u32[]{:S(2)}) collective-permute-start(bf16[256,512]{1,0:T(8,128)(2,1)S(1)} %collective-permute-done.5.vb), channel_id=1, source_target_pairs={{0,4},{1,61},{2,6},{3,63},{4,8},{5,1},{6,10},{7,3},{8,12},{9,5},{1... | collective-permute-start | bytes 786440 | tf_op jit(solution)/shard_map/ppermute | solution.py:38
  37.2 14.6 %collective-permute-start.6 = (bf16[256,512]{1,0:T(8,128)(2,1)S(1)}, bf16[256,512]{1,0:T(8,128)(2,1)S(1)}, u32[]{:S(2)}, u32[]{:S(2)}) collective-permute-start(bf16[256,512]{1,0:T(8,128)(2,1)S(1)} %collective-permute-done.2.kb), channel_id=1, source_target_pairs={{0,4},{1,61},{2,6},{3,63},{4,8},{5,1},{6,10},{7,3},{8,12},{9,5},{1... | collective-permute-start | bytes 786440 | tf_op jit(solution)/shard_map/ppermute | solution.py:38
  39.4 14.1 %collective-permute-start.4 = (bf16[256,512]{1,0:T(8,128)(2,1)S(1)}, bf16[256,512]{1,0:T(8,128)(2,1)S(1)}, u32[]{:S(2)}, u32[]{:S(2)}) collective-permute-start(bf16[256,512]{1,0:T(8,128)(2,1)S(1)} %get-tuple-element.28), channel_id=1, source_target_pairs={{0,64},{1,65},{2,66},{3,67},{4,68},{5,69},{6,70},{7,71},{8,72},{9,... | collective-permute-start | bytes 786440 | tf_op jit(solution)/shard_map/ppermute | solution.py:38
  40.7 15.0 %collective-permute-start.3 = (bf16[256,512]{1,0:T(8,128)(2,1)S(1)}, bf16[256,512]{1,0:T(8,128)(2,1)S(1)}, u32[]{:S(2)}, u32[]{:S(2)}) collective-permute-start(bf16[256,512]{1,0:T(8,128)(2,1)S(1)} %collective-permute-done.2.kb), channel_id=1, source_target_pairs={{0,67},{1,66},{2,65},{3,64},{4,71},{5,70},{6,69},{7,68},{8,75},{9,... | collective-permute-start | bytes 786440 | tf_op jit(solution)/shard_map/ppermute | solution.py:38

commit v3 on v2

v3 whole, which is shorter than its diff:
```python
import math

import jax
import jax.numpy as jnp
from jax import lax
from jax.experimental import pallas as pl
from jax.experimental.pallas import tpu as pltpu
from jax.sharding import PartitionSpec as P


HEADS = 8
HEAD_DIM = 64
TILE = 128
TILES = 4
LISTED = 6
BOUNDARY = 4
EXTRA = 16
PAIRS = 4
BATCH = 4
WIDTH = HEADS * HEAD_DIM
AXES = ("group", "slab")
SCALE = HEAD_DIM ** (-0.5) * math.log2(math.e)
LOWEST = -1e30

VMEM = pl.BlockSpec(memory_space=pltpu.VMEM)
ANY = pl.BlockSpec(memory_space=pl.ANY)
SMEM = pl.BlockSpec(memory_space=pltpu.SMEM)


def move(block, target):
    groups, slabs = lax.axis_size("group"), lax.axis_size("slab")
    route = []
    for g in range(groups):
        for s in range(slabs):
            to_g, to_s = target(g, s)
            route.append((g * slabs + s, (to_g % groups) * slabs + to_s % slabs))
    return lax.ppermute(block, AXES, route)


def to_chip(g, s):
    return g, s ^ 1


def to_cross(g, s):
    return g, s ^ 3


def to_forward(g, s):
    return 1 - g, s ^ 3


def to_along(g, s):
    return g, (s + 4 if s % 2 == 0 else s - 4)


def to_other(g, s):
    return g, (s - 1 if s % 2 == 0 else s + 1)


def keys_kernel(keys, *refs):
    *chunks, sems = refs
    copies = [
        pltpu.make_async_copy(keys.at[pl.ds(start, chunk.shape[0])], chunk, sems.at[i])
        for i, (start, chunk) in enumerate(zip((0, TILE, 2 * TILE), chunks))
    ]
    for copy in copies:
        copy.start()
    for copy in copies:
        copy.wait()


def split_keys(keys):
    return pl.pallas_call(
        keys_kernel,
        out_shape=[jax.ShapeDtypeStruct((n * TILE, WIDTH), keys.dtype) for n in (1, 1, 2)],
        in_specs=[ANY],
        out_specs=[VMEM] * 3,
        scratch_shapes=[pltpu.SemaphoreType.DMA((3,))],
        compiler_params=pltpu.CompilerParams(vmem_limit_bytes=2 << 20),
        cost_estimate=pl.CostEstimate(flops=400_000_000, bytes_accessed=8 << 20, transcendentals=0),
        name="split_keys",
    )(keys)


def prepare_kernel(q_ref, v_ref, ids, v_first, v_second, v_all, w_ref):
    lane = lax.broadcasted_iota(jnp.int32, (EXTRA, WIDTH), 1)
    row = jnp.zeros((EXTRA, WIDTH), jnp.int32)
    for j in range(BOUNDARY):
        row = jnp.where(lane == j, ids[0, j], row)
    v_first[2 * TILE :] = row.astype(jnp.float32).astype(jnp.bfloat16)
    for t in range(TILES):
        rows = pl.ds(t * TILE, TILE)
        part = (v_first, v_second)[t // 2]
        for p in range(PAIRS):
            lanes = pl.ds(p * TILE, TILE)
            vt = v_ref[rows, lanes].T
            v_all[rows, lanes] = vt
            part[pl.ds(t % 2 * TILE, TILE), lanes] = vt
            qt = q_ref[rows, lanes].T
            zero = jnp.zeros((HEAD_DIM, TILE), jnp.bfloat16)
            w_ref[t, p, :HEAD_DIM, :TILE] = qt[:HEAD_DIM]
            w_ref[t, p, :HEAD_DIM, TILE:] = zero
            w_ref[t, p, HEAD_DIM:, :TILE] = zero
            w_ref[t, p, HEAD_DIM:, TILE:] = qt[HEAD_DIM:]


def prepare(q, v, ids):
    half = 2 * TILE
    shapes = [(half + EXTRA, WIDTH), (half, WIDTH), v.shape, (TILES, PAIRS, TILE, 2 * TILE)]
    return pl.pallas_call(
        prepare_kernel,
        out_shape=[jax.ShapeDtypeStruct(shape, v.dtype) for shape in shapes],
        in_specs=[VMEM, VMEM, SMEM],
        out_specs=[VMEM] * 4,
        compiler_params=pltpu.CompilerParams(vmem_limit_bytes=8 << 20),
        cost_estimate=flops(1),
        name="prepare",
    )(q, v, ids)


def list_items(lists_ref, live, source_of, items):
    count = jnp.int32(0)
    for t in range(TILES):
        for j in range(LISTED):
            here, tile = source_of(lists_ref[t, j])
            items[count] = t * 16 + tile
            count = count + jnp.where(jnp.logical_and(here, t < live), 1, 0)
    for j in range(BATCH - 1):
        items[count + j] = TILES * 16
    return count


def attend_batch(first, size, items, k_ref, v_ref, w_ref, acc, peak, total):
    for u in range(size):
        item = items[first + u]
        t = lax.div(item, jnp.int32(16))
        rows = pl.ds(pl.multiple_of(lax.rem(item, jnp.int32(16)) * TILE, TILE), TILE)
        tq = jnp.minimum(t, TILES - 1)
        tops, sums, mixes = [], [], []
        for p in range(PAIRS):
            lanes = pl.ds(p * TILE, TILE)
            scores = jnp.dot(k_ref[rows, lanes], w_ref[tq, p], preferred_element_type=jnp.float32)
            top = jnp.max(scores, axis=0, keepdims=True)
            weights = jnp.exp2(scores * SCALE - top * SCALE)
            add = jnp.sum(weights, axis=0, keepdims=True)
            weights = weights.astype(jnp.bfloat16)
            vt = v_ref[rows, lanes]
            for h in range(2):
                half = slice(h * TILE, (h + 1) * TILE)
                tops.append(top[:, half])
                sums.append(add[:, half])
                mixes.append(
                    jnp.dot(
                        vt[h * HEAD_DIM : (h + 1) * HEAD_DIM],
                        weights[:, half],
                        preferred_element_type=jnp.float32,
                    )
                )
        top = jnp.concatenate(tops, axis=0)
        add = jnp.concatenate(sums, axis=0)
        old = peak[t]
        new = jnp.maximum(old, top)
        keep = jnp.exp2((old - new) * SCALE)
        take = jnp.exp2((top - new) * SCALE)
        peak[t] = new
        total[t] = total[t] * keep + add * take
        for h in range(HEADS):
            dims = pl.ds(h * HEAD_DIM, HEAD_DIM)
            acc[t, dims] = acc[t, dims] * keep[h : h + 1] + mixes[h] * take[h : h + 1]


def attend_items(count, items, *refs):
    whole = lax.div(count + (BATCH // 2 - 1), jnp.int32(BATCH))

    def batch(b, carry):
        attend_batch(b * BATCH, BATCH, items, *refs)
        return carry

    lax.fori_loop(0, whole, batch, 0)

    @pl.when(count > whole * BATCH)
    def _():
        attend_batch(whole * BATCH, BATCH // 2, items, *refs)


def first_kernel(lists, live, k_ref, v_ref, b0, b1, w_ref, acc, peak, total, joined, items):
    joined[:TILE] = b0[...]
    joined[TILE:] = b1[...]
    acc[...] = jnp.zeros_like(acc)
    peak[...] = jnp.full_like(peak, LOWEST)
    total[...] = jnp.zeros_like(total)
    count = list_items(lists, live[0], lambda pos: (pos < TILES, lax.rem(pos, 4)), items)
    attend_items(count, items, k_ref, v_ref, w_ref, acc, peak, total)


STATE = (
    jax.ShapeDtypeStruct((TILES + 1, WIDTH, TILE), jnp.float32),
    jax.ShapeDtypeStruct((TILES + 1, HEADS, TILE), jnp.float32),
    jax.ShapeDtypeStruct((TILES + 1, HEADS, TILE), jnp.float32),
)
ITEMS = pltpu.SMEM((TILES * LISTED + BATCH,), jnp.int32)


def flops(items):
    return pl.CostEstimate(flops=items * 40_000_000, bytes_accessed=1 << 20, transcendentals=0)


def first_stage(lists, live, k, v, b0, b1, w):
    return pl.pallas_call(
        first_kernel,
        out_shape=STATE + (jax.ShapeDtypeStruct((2 * TILE, WIDTH), k.dtype),),
        in_specs=[SMEM, SMEM] + [VMEM] * 5,
        out_specs=(VMEM,) * 4,
        scratch_shapes=[ITEMS],
        compiler_params=pltpu.CompilerParams(vmem_limit_bytes=16 << 20),
        cost_estimate=flops(8),
        name="first_stage",
    )(lists, live, k, v, b0, b1, w)


def is_inner():
    at = lax.rem(lax.axis_index("slab"), 4)
    return jnp.logical_or(at == 1, at == 2)


def is_odd():
    return lax.rem(lax.axis_index("slab"), 2) == 1


def find_near():
    base = jnp.where(is_odd(), TILES, 2 * TILES)

    def find(pos):
        at = pos - base
        here = jnp.logical_and(at >= 0, at < TILES)
        return here, jnp.where(here, at, 0)

    return find


def find_other(half):
    base = jnp.where(is_odd(), 2 * TILES, TILES) + 2 * half

    def find(pos):
        at = pos - base
        here = jnp.logical_and(at >= 0, at < 2)
        return here, jnp.where(here, at, 0)

    return find


def find_far(marks, half):
    lane = lax.broadcasted_iota(jnp.int32, (1, TILE), 1)
    line = marks[2 * TILE : 2 * TILE + EXTRA, :TILE].astype(jnp.float32)[:1]
    ids = [jnp.sum(jnp.where(lane == j, line, 0.0)).astype(jnp.int32) for j in range(BOUNDARY)]

    def find(pos):
        at = jnp.int32(-1)
        for j in range(BOUNDARY):
            at = jnp.where(pos == 3 * TILES + j, ids[j] - 2 * half, at)
        here = jnp.logical_and(at >= 0, at < 2)
        return here, jnp.where(here, at, 0)

    return find


def near_kernel(lists, live, k_ref, v_ref, w_ref, acc0, peak0, total0, acc, peak, total, items):
    count = list_items(lists, live[0], find_near(), items)
    attend_items(count, items, k_ref, v_ref, w_ref, acc, peak, total)


def attend_other(half, lists, live, kb, vb, kd, vd, w_ref, acc, peak, total, items):
    count = list_items(lists, live[0], find_other(half), items)

    @pl.when(is_inner())
    def _():
        attend_items(count, items, kb, vb, w_ref, acc, peak, total)

    @pl.when(jnp.logical_not(is_inner()))
    def _():
        attend_items(count, items, kd, vd, w_ref, acc, peak, total)


def attend_far(half, marks, lists, live, k_ref, v_ref, w_ref, acc, peak, total, items):
    count = list_items(lists, live[0], find_far(marks, half), items)
    attend_items(count, items, k_ref, v_ref, w_ref, acc, peak, total)


def middle_kernel(lists, live, kb, vb, kd, vd, kc0, kc1, vc, w_ref, acc0, peak0, total0, acc, peak, total, items, kc):
    kc[:TILE] = kc0[...]
    kc[TILE:] = kc1[...]
    attend_far(0, vc, lists, live, kc, vc, w_ref, acc, peak, total, items)
    attend_other(0, lists, live, kb, vb, kd, vd, w_ref, acc, peak, total, items)


def stage(kernel, lists, live, tiles, w, state, extra=(), scratch=()):
    args = (lists, live, *tiles, w, *state)
    first = len(args) - 3
    return pl.pallas_call(
        kernel,
        out_shape=STATE + tuple(extra),
        in_specs=[SMEM] * 2 + [VMEM] * (len(args) - 2),
        out_specs=(VMEM,) * (3 + len(extra)),
        input_output_aliases={first: 0, first + 1: 1, first + 2: 2},
        scratch_shapes=[ITEMS, *scratch],
        compiler_params=pltpu.CompilerParams(vmem_limit_bytes=12 << 20),
        cost_estimate=flops(8),
    )(*args)


def last_kernel(lists, live, marks, kb, vb, kd, vd, kc, vc, w_ref, acc, peak, total, out, items):
    attend_far(1, marks, lists, live, kc, vc, w_ref, acc, peak, total, items)
    attend_other(1, lists, live, kb, vb, kd, vd, w_ref, acc, peak, total, items)
    for t in range(TILES):
        rows = pl.ds(t * TILE, TILE)

        @pl.when(t < live[0])
        def _():
            share = 1.0 / total[t]
            for p in range(PAIRS):
                halves = [
                    acc[t, pl.ds((2 * p + h) * HEAD_DIM, HEAD_DIM)] * share[2 * p + h : 2 * p + h + 1]
                    for h in range(2)
                ]
                mixed = jnp.concatenate(halves, axis=0).astype(jnp.bfloat16)
                out[rows, pl.ds(p * TILE, TILE)] = mixed.T

        @pl.when(t >= live[0])
        def _():
            out[rows] = jnp.zeros((TILE, WIDTH), jnp.bfloat16)


def last_stage(lists, live, tiles, w, state):
    return pl.pallas_call(
        last_kernel,
        out_shape=jax.ShapeDtypeStruct((TILES * TILE, WIDTH), jnp.bfloat16),
        in_specs=[SMEM] * 2 + [VMEM] * 11,
        out_specs=VMEM,
        scratch_shapes=[ITEMS],
        compiler_params=pltpu.CompilerParams(vmem_limit_bytes=12 << 20),
        cost_estimate=flops(8),
        name="last_stage",
    )(lists, live, *tiles, w, *state)


def shards(queries, keys, values, neighbours, live_tiles, boundary_ids):
    keys_in = split_keys(keys)
    va, vz, vt, w = prepare(queries, values, boundary_ids)
    common = neighbours, live_tiles
    pair = jax.ShapeDtypeStruct((2 * TILE, WIDTH), keys.dtype)
    near = move(keys, to_chip), move(vt, to_chip)
    k0, k1, kz = keys_in
    cross = [move(x, to_cross) for x in (k0, k1, va, vz)]
    far = [move(x, to_forward) for x in cross]
    far_last = move(move(kz, to_forward), to_cross)
    other_last = move(kz, to_other)
    *state, joined = first_stage(*common, keys, vt, cross[0], cross[1], w)
    state = stage(near_kernel, *common, near, w, state)
    along = [move(x, to_along) for x in (joined, cross[2], cross[3])]
    tiles = joined, cross[2], along[0], along[1], far[0], far[1], far[2]
    scratch = (pltpu.VMEM(pair.shape, pair.dtype),)
    state = stage(middle_kernel, *common, tiles, w, state, scratch=scratch)
    tiles = far[2], other_last, cross[3], other_last, along[2], far_last, far[3]
    return last_stage(*common, tiles, w, state)


def solution(mesh):
    spec = P(AXES, None)
    return jax.shard_map(
        shards,
        mesh=mesh,
        in_specs=(spec, spec, spec, spec, P(AXES), spec),
        out_specs=spec,
        check_vma=False,
    )
```

time: 59 us -> 56.2 us (0.953)
  waiting for transfers between devices: 21 us -> 12.9 us
  starting transfers between devices: 23.9 us -> 30.8 us
  Pallas kernels: 11.1 us -> 9.56 us
    ppermute x14 -> x16, waiting for transfers between devices: 21 us -> 12.9 us  [move(): return lax.ppermute(block, AXES, route)]
    ppermute x14 -> x16, starting transfers between devices: 23.9 us -> 30.8 us  [move(): return lax.ppermute(block, AXES, route)]
    pallas_call x6 -> x4, Pallas kernels: 7.31 us -> 5.41 us  [the longest x2 3.68 us: stage(): pl.pallas_call(kernel, out_shape=STATE + tuple(extra), in_specs=[SMEM] *...]
  transfers between devices with their start and end apart: 14 -> 16, of which waited for: 5 -> 5; matrix products, arithmetic and copies ran while one was open for 0% -> 0% of each run, Pallas kernels for 14% -> 11%
where the time goes in v3:
time: 56.2 us; the launch traced here: 55.9 us
  starting transfers between devices  30.8 us (55%)
  waiting for transfers between devices  12.9 us (23%)
  Pallas kernels  9.56 us (17%)
  local copies, waits for them, and re-layouts  1.8 us (3%)
  between operations  0.77 us (1%)
    ppermute x16, starting transfers between devices, move(): return lax.ppermute(block, AXES, route)  30.8 us
    ppermute x16, waiting for transfers between devices, move(): return lax.ppermute(block, AXES, route)  12.9 us
    pallas_call x2, Pallas kernels, stage(): pl.pallas_call(kernel, out_shape=STATE + tuple(extra), in_specs=[SMEM] *...  3.68 us
    pallas_call x1, Pallas kernels, last_stage(): pl.pallas_call(last_kernel, out_shape=jax.ShapeDtypeStruct((TILES * TILE,...  3.24 us
    unnamed x12, local copies, waits for them, and re-layouts  1.8 us
    pallas_call x1, Pallas kernels, first_stage(): pl.pallas_call(first_kernel, out_shape=STATE + (jax.ShapeDtypeStruct((2 *...  1.35 us
  transfers between devices with their start and end apart: 16, of which 5 were waited for; matrix products, arithmetic and copies ran while one was open for 0% of the time, Pallas kernels for 11%

profile of v3, /device:TPU:1, one launch (start us, length us, event | category | flops | bytes accessed | tf_op | source)
XLA Modules:
  0.0 55.9 jit_solution(3354155391546901949)
XLA Ops:
  0.0 0.0 copy-start
  0.0 0.0 copy-start.1
  0.0 0.0 copy-start.2
  0.0 1.1 %copy-done.2 = bf16[512,512]{1,0:T(8,128)(2,1)S(1)} copy-done((bf16[512,512]{1,0:T(8,128)(2,1)S(1)}, bf16[512,512]{1,0:T(8,128)(2,1)}, u32[]{:S(2)}) %copy-start.2) | copy-done | bytes 524312
  1.1 0.0 copy-start.3
  1.1 0.0 copy-start.4
  1.1 0.4 split_keys.1
  1.5 3.1 %collective-permute-start.8 = (bf16[128,512]{1,0:T(8,128)(2,1)S(1)}, bf16[128,512]{1,0:T(8,128)(2,1)S(1)}, u32[]{:S(2)}, u32[]{:S(2)}) collective-permute-start(bf16[128,512]{1,0:T(8,128)(2,1)S(1)} %get-tuple-element.27), channel_id=1, source_target_pairs={{0,3},{1,2},{2,1},{3,0},{4,7},{5,6},{6,5},{7,4},{8,11},{9,10},{10,... | collective-permute-start | bytes 393224 | tf_op jit(solution)/shard_map/ppermute | solution.py:37
  4.6 0.1 collective-permute-start.9
  4.7 0.0 copy-done
  4.7 0.0 copy-done.1
  4.7 0.0 copy-start.5
  4.7 0.7 %copy-done.5 = s32[1,4]{1,0:T(1,128)S(1)} copy-done((s32[1,4]{1,0:T(1,128)S(1)}, s32[1,4]{1,0:T(1,128)}, u32[]{:S(2)}) %copy-start.5) | copy-done | bytes 40
  5.4 0.9 %prepare.1 = (bf16[272,512]{1,0:T(8,128)(2,1)S(1)}, bf16[256,512]{1,0:T(8,128)(2,1)S(1)}, bf16[512,512]{1,0:T(8,128)(2,1)S(1)}, bf16[4,4,128,256]{3,2,1,0:T(8,128)(2,1)S(1)}) custom-call(bf16[512,512]{1,0:T(8,128)(2,1)S(1)} %copy-done, bf16[512,512]{1,0:T(8,128)(2,1)S(1)} %copy-done.1, s32[1,4]{1,0:T(1,128)S(1)} %copy-done.5), custom_call_target="tpu_custom_call" | custom-call | flops 40000000 | bytes 1048576 | tf_op jit(solution)/shard_map/prepare/pallas_call | solution.py:110
  6.3 1.7 %collective-permute-start = (bf16[272,512]{1,0:T(8,128)(2,1)S(1)}, bf16[272,512]{1,0:T(8,128)(2,1)S(1)}, u32[]{:S(2)}, u32[]{:S(2)}) collective-permute-start(bf16[272,512]{1,0:T(8,128)(2,1)S(1)} %get-tuple-element.22), channel_id=1, source_target_pairs={{0,3},{1,2},{2,1},{3,0},{4,7},{5,6},{6,5},{7,4},{8,11},{9,10},{10,... | collective-permute-start | bytes 835592 | tf_op jit(solution)/shard_map/ppermute | solution.py:37
  8.0 0.9 %collective-permute-done.8.b0 = bf16[128,512]{1,0:T(8,128)(2,1)S(1)} collective-permute-done((bf16[128,512]{1,0:T(8,128)(2,1)S(1)}, bf16[128,512]{1,0:T(8,128)(2,1)S(1)}, u32[]{:S(2)}, u32[]{:S(2)}) %collective-permute-start.8) | collective-permute-done | bytes 131104 | tf_op jit(solution)/shard_map/ppermute | solution.py:37
  9.0 3.6 %collective-permute-start.12 = (bf16[128,512]{1,0:T(8,128)(2,1)S(1)}, bf16[128,512]{1,0:T(8,128)(2,1)S(1)}, u32[]{:S(2)}, u32[]{:S(2)}) collective-permute-start(bf16[128,512]{1,0:T(8,128)(2,1)S(1)} %collective-permute-done.8.b0), channel_id=1, source_target_pairs={{0,67},{1,66},{2,65},{3,64},{4,71},{5,70},{6,69},{7,68},{8,75},{9,... | collective-permute-start | bytes 393224 | tf_op jit(solution)/shard_map/ppermute | solution.py:37
  12.5 0.0 collective-permute-start.3
  12.5 0.1 collective-permute-start.15
  12.7 0.0 collective-permute-done.9.b1
  12.7 0.0 copy-done.3
  12.7 0.4 collective-permute-start.14
  13.0 3.0 %collective-permute-done.12.kc0 = bf16[128,512]{1,0:T(8,128)(2,1)S(1)} collective-permute-done((bf16[128,512]{1,0:T(8,128)(2,1)S(1)}, bf16[128,512]{1,0:T(8,128)(2,1)S(1)}, u32[]{:S(2)}, u32[]{:S(2)}) %collective-permute-start.12) | collective-permute-done | bytes 131104 | tf_op jit(solution)/shard_map/ppermute | solution.py:37
  16.0 3.2 %collective-permute-start.13 = (bf16[128,512]{1,0:T(8,128)(2,1)S(1)}, bf16[128,512]{1,0:T(8,128)(2,1)S(1)}, u32[]{:S(2)}, u32[]{:S(2)}) collective-permute-start(bf16[128,512]{1,0:T(8,128)(2,1)S(1)} %collective-permute-done.9.b1), channel_id=1, source_target_pairs={{0,67},{1,66},{2,65},{3,64},{4,71},{5,70},{6,69},{7,68},{8,75},{9,... | collective-permute-start | bytes 393224 | tf_op jit(solution)/shard_map/ppermute | solution.py:37
  19.2 3.5 %collective-permute-done.13.kc1 = bf16[128,512]{1,0:T(8,128)(2,1)S(1)} collective-permute-done((bf16[128,512]{1,0:T(8,128)(2,1)S(1)}, bf16[128,512]{1,0:T(8,128)(2,1)S(1)}, u32[]{:S(2)}, u32[]{:S(2)}) %collective-permute-start.13) | collective-permute-done | bytes 131104 | tf_op jit(solution)/shard_map/ppermute | solution.py:37
  22.7 3.2 %collective-permute-start.5 = (bf16[256,512]{1,0:T(8,128)(2,1)S(1)}, bf16[256,512]{1,0:T(8,128)(2,1)S(1)}, u32[]{:S(2)}, u32[]{:S(2)}) collective-permute-start(bf16[256,512]{1,0:T(8,128)(2,1)S(1)} %get-tuple-element.23), channel_id=1, source_target_pairs={{0,67},{1,66},{2,65},{3,64},{4,71},{5,70},{6,69},{7,68},{8,75},{9,... | collective-permute-start | bytes 786440 | tf_op jit(solution)/shard_map/ppermute | solution.py:37
  26.5 0.0 collective-permute-done.vb
  26.5 0.1 collective-permute-start.1
  26.6 0.0 copy-done.4
  26.6 1.4 %first_stage.1 = (f32[5,512,128]{2,1,0:T(8,128)S(1)}, f32[5,8,128]{2,1,0:T(8,128)S(1)}, f32[5,8,128]{2,1,0:T(8,128)S(1)}, bf16[256,512]{1,0:T(8,128)(2,1)S(1)}) custom-call(s32[4,6]{1,0:T(4,128)S(1)} %copy-done.4, s32[1]{0:T(128)S(6)} %copy.19.live, bf16[512,512]{1,0:T(8,128)(2,1)S(1)} %copy-done.3, bf16[512,512]{1,0:T(8,128)(2,1)S(1)} %get-tuple-element.26.v_ref, ...), custom_call_target="tpu_custom_call" | custom-call | flops 320000000 | bytes 1048576 | tf_op jit(solution)/shard_map/first_stage/pallas_call | solution.py:209
  28.0 0.0 collective-permute-done.3.vb
  28.0 5.0 %collective-permute-start.10 = (bf16[256,512]{1,0:T(8,128)(2,1)S(1)}, bf16[256,512]{1,0:T(8,128)(2,1)S(1)}, u32[]{:S(2)}, u32[]{:S(2)}) collective-permute-start(bf16[256,512]{1,0:T(8,128)(2,1)S(1)} %get-tuple-element.29.kb), channel_id=1, source_target_pairs={{0,4},{1,61},{2,6},{3,63},{4,8},{5,1},{6,10},{7,3},{8,12},{9,5},{1... | collective-permute-start | bytes 786440 | tf_op jit(solution)/shard_map/ppermute | solution.py:37
  33.0 0.0 collective-permute-done.5
  33.0 4.9 %collective-permute-start.11 = (bf16[272,512]{1,0:T(8,128)(2,1)S(1)}, bf16[272,512]{1,0:T(8,128)(2,1)S(1)}, u32[]{:S(2)}, u32[]{:S(2)}) collective-permute-start(bf16[272,512]{1,0:T(8,128)(2,1)S(1)} %collective-permute-done.vb), channel_id=1, source_target_pairs={{0,4},{1,61},{2,6},{3,63},{4,8},{5,1},{6,10},{7,3},{8,12},{9,5},{1... | collective-permute-start | bytes 835592 | tf_op jit(solution)/shard_map/ppermute | solution.py:37
  38.0 0.0 collective-permute-done.10.kd
  38.0 0.0 collective-permute-start.2
  38.0 0.0 collective-permute-done.15.v_ref
  38.0 3.6 %collective-permute-start.4 = (bf16[256,512]{1,0:T(8,128)(2,1)S(1)}, bf16[256,512]{1,0:T(8,128)(2,1)S(1)}, u32[]{:S(2)}, u32[]{:S(2)}) collective-permute-start(bf16[256,512]{1,0:T(8,128)(2,1)S(1)} %collective-permute-done.3.vb), channel_id=1, source_target_pairs={{0,4},{1,61},{2,6},{3,63},{4,8},{5,1},{6,10},{7,3},{8,12},{9,5},{1... | collective-permute-start | bytes 786440 | tf_op jit(solution)/shard_map/ppermute | solution.py:37
  41.6 0.0 collective-permute-done.14.k_ref
  41.6 0.0 collective-permute-start.7
  41.6 0.0 collective-permute-done.1.vc.marks
  41.6 1.9 %collective-permute-start.6 = (bf16[256,512]{1,0:T(8,128)(2,1)S(1)}, bf16[256,512]{1,0:T(8,128)(2,1)S(1)}, u32[]{:S(2)}, u32[]{:S(2)}) collective-permute-start(bf16[256,512]{1,0:T(8,128)(2,1)S(1)} %collective-permute-done.5), channel_id=1, source_target_pairs={{0,3},{1,2},{2,1},{3,0},{4,7},{5,6},{6,5},{7,4},{8,11},{9,10},{10,... | collective-permute-start | bytes 786440 | tf_op jit(solution)/shard_map/ppermute | solution.py:37
  43.5 1.6 %shard_map.64 = (f32[5,512,128]{2,1,0:T(8,128)S(1)}, f32[5,8,128]{2,1,0:T(8,128)S(1)}, f32[5,8,128]{2,1,0:T(8,128)S(1)}) custom-call(s32[4,6]{1,0:T(4,128)S(1)} %copy-done.4, s32[1]{0:T(128)S(6)} %copy.19.live, bf16[512,512]{1,0:T(8,128)(2,1)S(1)} %collective-permute-done.14.k_ref, ...), custom_call_target="tpu_custom_call", output_to_operand_aliasing={{0}: (5, {}), {1}: (6, {}), {2}: (7, {})} | custom-call | flops 320000000 | bytes 1048576 | tf_op jit(solution)/shard_map/pallas_call | solution.py:299
  45.1 0.0 collective-permute-done.11.vd
  45.1 2.1 %shard_map.65 = (f32[5,512,128]{2,1,0:T(8,128)S(1)}, f32[5,8,128]{2,1,0:T(8,128)S(1)}, f32[5,8,128]{2,1,0:T(8,128)S(1)}) custom-call(s32[4,6]{1,0:T(4,128)S(1)} %copy-done.4, s32[1]{0:T(128)S(6)} %copy.19.live, bf16[256,512]{1,0:T(8,128)(2,1)S(1)} %get-tuple-element.29.kb, ...), custom_call_target="tpu_custom_call", output_to_operand_aliasing={{0}: (10, {}), {1}: (11, {}), {2}: (12, {})} | custom-call | flops 320000000 | bytes 1048576 | tf_op jit(solution)/shard_map/pallas_call | solution.py:299
  47.2 0.0 collective-permute-done.2.kb.kd
  47.2 0.0 collective-permute-done.4.vd
  47.2 4.0 %collective-permute-done.7.vc = bf16[256,512]{1,0:T(8,128)(2,1)S(1)} collective-permute-done((bf16[256,512]{1,0:T(8,128)(2,1)S(1)}, bf16[256,512]{1,0:T(8,128)(2,1)S(1)}, u32[]{:S(2)}, u32[]{:S(2)}) %collective-permute-start.7) | collective-permute-done | bytes 262176 | tf_op jit(solution)/shard_map/ppermute | solution.py:37
  51.2 1.5 %collective-permute-done.6.kc = bf16[256,512]{1,0:T(8,128)(2,1)S(1)} collective-permute-done((bf16[256,512]{1,0:T(8,128)(2,1)S(1)}, bf16[256,512]{1,0:T(8,128)(2,1)S(1)}, u32[]{:S(2)}, u32[]{:S(2)}) %collective-permute-start.6) | collective-permute-done | bytes 262176 | tf_op jit(solution)/shard_map/ppermute | solution.py:37
  52.6 3.2 %last_stage.1 = bf16[512,512]{1,0:T(8,128)(2,1)} custom-call(s32[4,6]{1,0:T(4,128)S(1)} %copy-done.4, s32[1]{0:T(128)S(6)} %copy.19.live, bf16[272,512]{1,0:T(8,128)(2,1)S(1)} %collective-permute-done.1.vc.marks, bf16[256,512]{1,0:T(8,128)(2,1)S(1)} %collective-permute-done.2.kb.kd, bf16[256,512]{1,0:T(8,128)(2,1)S(1)} %collective-permute-done.3.vb, ...), custom_call_target="tpu_custom_call" | custom-call | flops 320000000 | bytes 1048576 | tf_op jit(solution)/shard_map/last_stage/pallas_call | solution.py:334
Async XLA Ops:
  0.0 4.7 %copy-start = (bf16[512,512]{1,0:T(8,128)(2,1)S(1)}, bf16[512,512]{1,0:T(8,128)(2,1)}, u32[]{:S(2)}) copy-start(bf16[512,512]{1,0:T(8,128)(2,1)} %q_ref.1) | copy-start | bytes 1572868
  0.0 4.7 %copy-start.1 = (bf16[512,512]{1,0:T(8,128)(2,1)S(1)}, bf16[512,512]{1,0:T(8,128)(2,1)}, u32[]{:S(2)}) copy-start(bf16[512,512]{1,0:T(8,128)(2,1)} %v_ref.1) | copy-start | bytes 1572868
  0.0 1.1 %copy-start.2 = (bf16[512,512]{1,0:T(8,128)(2,1)S(1)}, bf16[512,512]{1,0:T(8,128)(2,1)}, u32[]{:S(2)}) copy-start(bf16[512,512]{1,0:T(8,128)(2,1)} %k_ref.1) | copy-start | bytes 1572868
  1.1 11.5 %copy-start.3 = (bf16[512,512]{1,0:T(8,128)(2,1)S(1)}, bf16[512,512]{1,0:T(8,128)(2,1)}, u32[]{:S(2)}) copy-start(bf16[512,512]{1,0:T(8,128)(2,1)} %k_ref.1) | copy-start | bytes 1572868
  1.1 25.5 %copy-start.4 = (s32[4,6]{1,0:T(4,128)S(1)}, s32[4,6]{1,0:T(4,128)}, u32[]{:S(2)}) copy-start(s32[4,6]{1,0:T(4,128)} %lists.7) | copy-start | bytes 292
  1.5 7.4 %collective-permute-start.8 = (bf16[128,512]{1,0:T(8,128)(2,1)S(1)}, bf16[128,512]{1,0:T(8,128)(2,1)S(1)}, u32[]{:S(2)}, u32[]{:S(2)}) collective-permute-start(bf16[128,512]{1,0:T(8,128)(2,1)S(1)} %get-tuple-element.27), channel_id=1, source_target_pairs={{0,3},{1,2},{2,1},{3,0},{4,7},{5,6},{6,5},{7,4},{8,11},{9,10},{10,... | collective-permute-start | bytes 393224 | tf_op jit(solution)/shard_map/ppermute | solution.py:37
  4.6 8.1 %collective-permute-start.9 = (bf16[128,512]{1,0:T(8,128)(2,1)S(1)}, bf16[128,512]{1,0:T(8,128)(2,1)S(1)}, u32[]{:S(2)}, u32[]{:S(2)}) collective-permute-start(bf16[128,512]{1,0:T(8,128)(2,1)S(1)} %get-tuple-element.28), channel_id=1, source_target_pairs={{0,3},{1,2},{2,1},{3,0},{4,7},{5,6},{6,5},{7,4},{8,11},{9,10},{10,... | collective-permute-start | bytes 393224 | tf_op jit(solution)/shard_map/ppermute | solution.py:37
  4.7 0.7 %copy-start.5 = (s32[1,4]{1,0:T(1,128)S(1)}, s32[1,4]{1,0:T(1,128)}, u32[]{:S(2)}) copy-start(s32[1,4]{1,0:T(1,128)} %ids.1) | copy-start | bytes 52
  6.3 20.2 %collective-permute-start = (bf16[272,512]{1,0:T(8,128)(2,1)S(1)}, bf16[272,512]{1,0:T(8,128)(2,1)S(1)}, u32[]{:S(2)}, u32[]{:S(2)}) collective-permute-start(bf16[272,512]{1,0:T(8,128)(2,1)S(1)} %get-tuple-element.22), channel_id=1, source_target_pairs={{0,3},{1,2},{2,1},{3,0},{4,7},{5,6},{6,5},{7,4},{8,11},{9,10},{10,... | collective-permute-start | bytes 835592 | tf_op jit(solution)/shard_map/ppermute | solution.py:37
  9.0 7.1 %collective-permute-start.12 = (bf16[128,512]{1,0:T(8,128)(2,1)S(1)}, bf16[128,512]{1,0:T(8,128)(2,1)S(1)}, u32[]{:S(2)}, u32[]{:S(2)}) collective-permute-start(bf16[128,512]{1,0:T(8,128)(2,1)S(1)} %collective-permute-done.8.b0), channel_id=1, source_target_pairs={{0,67},{1,66},{2,65},{3,64},{4,71},{5,70},{6,69},{7,68},{8,75},{9,... | collective-permute-start | bytes 393224 | tf_op jit(solution)/shard_map/ppermute | solution.py:37
  12.5 15.5 %collective-permute-start.3 = (bf16[256,512]{1,0:T(8,128)(2,1)S(1)}, bf16[256,512]{1,0:T(8,128)(2,1)S(1)}, u32[]{:S(2)}, u32[]{:S(2)}) collective-permute-start(bf16[256,512]{1,0:T(8,128)(2,1)S(1)} %get-tuple-element.24), channel_id=1, source_target_pairs={{0,3},{1,2},{2,1},{3,0},{4,7},{5,6},{6,5},{7,4},{8,11},{9,10},{10,... | collective-permute-start | bytes 786440 | tf_op jit(solution)/shard_map/ppermute | solution.py:37
  12.5 25.5 %collective-permute-start.15 = (bf16[512,512]{1,0:T(8,128)(2,1)S(1)}, bf16[512,512]{1,0:T(8,128)(2,1)S(1)}, u32[]{:S(2)}, u32[]{:S(2)}) collective-permute-start(bf16[512,512]{1,0:T(8,128)(2,1)S(1)} %get-tuple-element.26.v_ref), channel_id=1, source_target_pairs={{0,1},{1,0},{2,3},{3,2},{4,5},{5,4},{6,7},{7,6},{8,9},{9,8},{10,11... | collective-permute-start | bytes 1572872 | tf_op jit(solution)/shard_map/ppermute | solution.py:37
  12.7 28.9 %collective-permute-start.14 = (bf16[512,512]{1,0:T(8,128)(2,1)S(1)}, bf16[512,512]{1,0:T(8,128)(2,1)S(1)}, u32[]{:S(2)}, u32[]{:S(2)}) collective-permute-start(bf16[512,512]{1,0:T(8,128)(2,1)S(1)} %copy-done.3), channel_id=1, source_target_pairs={{0,1},{1,0},{2,3},{3,2},{4,5},{5,4},{6,7},{7,6},{8,9},{9,8},{10,11... | collective-permute-start | bytes 1572872 | tf_op jit(solution)/shard_map/ppermute | solution.py:37
  16.0 6.7 %collective-permute-start.13 = (bf16[128,512]{1,0:T(8,128)(2,1)S(1)}, bf16[128,512]{1,0:T(8,128)(2,1)S(1)}, u32[]{:S(2)}, u32[]{:S(2)}) collective-permute-start(bf16[128,512]{1,0:T(8,128)(2,1)S(1)} %collective-permute-done.9.b1), channel_id=1, source_target_pairs={{0,67},{1,66},{2,65},{3,64},{4,71},{5,70},{6,69},{7,68},{8,75},{9,... | collective-permute-start | bytes 393224 | tf_op jit(solution)/shard_map/ppermute | solution.py:37
  22.7 10.3 %collective-permute-start.5 = (bf16[256,512]{1,0:T(8,128)(2,1)S(1)}, bf16[256,512]{1,0:T(8,128)(2,1)S(1)}, u32[]{:S(2)}, u32[]{:S(2)}) collective-permute-start(bf16[256,512]{1,0:T(8,128)(2,1)S(1)} %get-tuple-element.23), channel_id=1, source_target_pairs={{0,67},{1,66},{2,65},{3,64},{4,71},{5,70},{6,69},{7,68},{8,75},{9,... | collective-permute-start | bytes 786440 | tf_op jit(solution)/shard_map/ppermute | solution.py:37
  26.5 15.0 %collective-permute-start.1 = (bf16[272,512]{1,0:T(8,128)(2,1)S(1)}, bf16[272,512]{1,0:T(8,128)(2,1)S(1)}, u32[]{:S(2)}, u32[]{:S(2)}) collective-permute-start(bf16[272,512]{1,0:T(8,128)(2,1)S(1)} %collective-permute-done.vb), channel_id=1, source_target_pairs={{0,67},{1,66},{2,65},{3,64},{4,71},{5,70},{6,69},{7,68},{8,75},{9,... | collective-permute-start | bytes 835592 | tf_op jit(solution)/shard_map/ppermute | solution.py:37
  28.0 10.0 %collective-permute-start.10 = (bf16[256,512]{1,0:T(8,128)(2,1)S(1)}, bf16[256,512]{1,0:T(8,128)(2,1)S(1)}, u32[]{:S(2)}, u32[]{:S(2)}) collective-permute-start(bf16[256,512]{1,0:T(8,128)(2,1)S(1)} %get-tuple-element.29.kb), channel_id=1, source_target_pairs={{0,4},{1,61},{2,6},{3,63},{4,8},{5,1},{6,10},{7,3},{8,12},{9,5},{1... | collective-permute-start | bytes 786440 | tf_op jit(solution)/shard_map/ppermute | solution.py:37
  33.0 12.0 %collective-permute-start.11 = (bf16[272,512]{1,0:T(8,128)(2,1)S(1)}, bf16[272,512]{1,0:T(8,128)(2,1)S(1)}, u32[]{:S(2)}, u32[]{:S(2)}) collective-permute-start(bf16[272,512]{1,0:T(8,128)(2,1)S(1)} %collective-permute-done.vb), channel_id=1, source_target_pairs={{0,4},{1,61},{2,6},{3,63},{4,8},{5,1},{6,10},{7,3},{8,12},{9,5},{1... | collective-permute-start | bytes 835592 | tf_op jit(solution)/shard_map/ppermute | solution.py:37
  38.0 9.2 %collective-permute-start.2 = (bf16[256,512]{1,0:T(8,128)(2,1)S(1)}, bf16[256,512]{1,0:T(8,128)(2,1)S(1)}, u32[]{:S(2)}, u32[]{:S(2)}) collective-permute-start(bf16[256,512]{1,0:T(8,128)(2,1)S(1)} %get-tuple-element.23), channel_id=1, source_target_pairs={{0,63},{1,2},{2,1},{3,4},{4,3},{5,6},{6,5},{7,8},{8,7},{9,10},{10,... | collective-permute-start | bytes 786440 | tf_op jit(solution)/shard_map/ppermute | solution.py:37
  38.0 9.2 %collective-permute-start.4 = (bf16[256,512]{1,0:T(8,128)(2,1)S(1)}, bf16[256,512]{1,0:T(8,128)(2,1)S(1)}, u32[]{:S(2)}, u32[]{:S(2)}) collective-permute-start(bf16[256,512]{1,0:T(8,128)(2,1)S(1)} %collective-permute-done.3.vb), channel_id=1, source_target_pairs={{0,4},{1,61},{2,6},{3,63},{4,8},{5,1},{6,10},{7,3},{8,12},{9,5},{1... | collective-permute-start | bytes 786440 | tf_op jit(solution)/shard_map/ppermute | solution.py:37
  41.6 9.6 %collective-permute-start.7 = (bf16[256,512]{1,0:T(8,128)(2,1)S(1)}, bf16[256,512]{1,0:T(8,128)(2,1)S(1)}, u32[]{:S(2)}, u32[]{:S(2)}) collective-permute-start(bf16[256,512]{1,0:T(8,128)(2,1)S(1)} %collective-permute-done.3.vb), channel_id=1, source_target_pairs={{0,67},{1,66},{2,65},{3,64},{4,71},{5,70},{6,69},{7,68},{8,75},{9,... | collective-permute-start | bytes 786440 | tf_op jit(solution)/shard_map/ppermute | solution.py:37
  41.6 11.1 %collective-permute-start.6 = (bf16[256,512]{1,0:T(8,128)(2,1)S(1)}, bf16[256,512]{1,0:T(8,128)(2,1)S(1)}, u32[]{:S(2)}, u32[]{:S(2)}) collective-permute-start(bf16[256,512]{1,0:T(8,128)(2,1)S(1)} %collective-permute-done.5), channel_id=1, source_target_pairs={{0,3},{1,2},{2,1},{3,0},{4,7},{5,6},{6,5},{7,4},{8,11},{9,10},{10,... | collective-permute-start | bytes 786440 | tf_op jit(solution)/shard_map/ppermute | solution.py:37

commit v4 on v3

--- a/solution.py
+++ b/solution.py
@@ -308,35 +308,36 @@
     )(*args)
 
 
-def last_kernel(lists, live, marks, kb, vb, kd, vd, kc, vc, w_ref, acc, peak, total, out, items):
+def far_kernel(lists, live, marks, kc, vc, w_ref, acc0, peak0, total0, acc, peak, total, items):
     attend_far(1, marks, lists, live, kc, vc, w_ref, acc, peak, total, items)
+
+
+def last_kernel(lists, live, kb, vb, kd, vd, w_ref, acc, peak, total, out, items, done, sems):
     attend_other(1, lists, live, kb, vb, kd, vd, w_ref, acc, peak, total, items)
+    copies = []
     for t in range(TILES):
         rows = pl.ds(t * TILE, TILE)
-
-        @pl.when(t < live[0])
-        def _():
-            share = 1.0 / total[t]
-            for p in range(PAIRS):
-                halves = [
-                    acc[t, pl.ds((2 * p + h) * HEAD_DIM, HEAD_DIM)] * share[2 * p + h : 2 * p + h + 1]
-                    for h in range(2)
-                ]
-                mixed = jnp.concatenate(halves, axis=0).astype(jnp.bfloat16)
-                out[rows, pl.ds(p * TILE, TILE)] = mixed.T
-
-        @pl.when(t >= live[0])
-        def _():
-            out[rows] = jnp.zeros((TILE, WIDTH), jnp.bfloat16)
+        share = jnp.where(t < live[0], 1.0 / total[t], 0.0)
+        for p in range(PAIRS):
+            halves = [
+                acc[t, pl.ds((2 * p + h) * HEAD_DIM, HEAD_DIM)] * share[2 * p + h : 2 * p + h + 1]
+                for h in range(2)
+            ]
+            mixed = jnp.concatenate(halves, axis=0).astype(jnp.bfloat16)
+            done[rows, pl.ds(p * TILE, TILE)] = mixed.T
+        copies.append(pltpu.make_async_copy(done.at[rows], out.at[rows], sems.at[t]))
+        copies[-1].start()
+    for copy in copies:
+        copy.wait()
 
 
 def last_stage(lists, live, tiles, w, state):
     return pl.pallas_call(
         last_kernel,
         out_shape=jax.ShapeDtypeStruct((TILES * TILE, WIDTH), jnp.bfloat16),
-        in_specs=[SMEM] * 2 + [VMEM] * 11,
-        out_specs=VMEM,
-        scratch_shapes=[ITEMS],
+        in_specs=[SMEM] * 2 + [VMEM] * 8,
+        out_specs=ANY,
+        scratch_shapes=[ITEMS, pltpu.VMEM((TILES * TILE, WIDTH), jnp.bfloat16), pltpu.SemaphoreType.DMA((TILES,))],
         compiler_params=pltpu.CompilerParams(vmem_limit_bytes=12 << 20),
         cost_estimate=flops(8),
         name="last_stage",
@@ -360,7 +361,8 @@
     tiles = joined, cross[2], along[0], along[1], far[0], far[1], far[2]
     scratch = (pltpu.VMEM(pair.shape, pair.dtype),)
     state = stage(middle_kernel, *common, tiles, w, state, scratch=scratch)
-    tiles = far[2], other_last, cross[3], other_last, along[2], far_last, far[3]
+    state = stage(far_kernel, *common, (far[2], far_last, far[3]), w, state)
+    tiles = other_last, cross[3], other_last, along[2]
     return last_stage(*common, tiles, w, state)
 
 

time: 56.2 us -> 55.4 us (0.986)
  starting transfers between devices: 30.8 us -> 29 us
    ppermute x16, starting transfers between devices: 30.8 us -> 29 us  [move(): return lax.ppermute(block, AXES, route)]
    pallas_call x2 -> x3, Pallas kernels: 3.68 us -> 5.19 us  [stage(): pl.pallas_call(kernel, out_shape=STATE + tuple(extra), in_specs=[SMEM] *...]
    pallas_call x1, Pallas kernels: 3.24 us -> 2.2 us  [last_stage(): pl.pallas_call(last_kernel, out_shape=jax.ShapeDtypeStruct((TILES * TILE,...]
  transfers between devices with their start and end apart: 16 -> 16, of which waited for: 5 -> 5; matrix products, arithmetic and copies ran while one was open for 0% -> 0% of each run, Pallas kernels for 11% -> 14%
where the time goes in v4:
time: 55.4 us; the launch traced here: 55 us
  starting transfers between devices  29 us (52%)
  waiting for transfers between devices  13.3 us (24%)
  Pallas kernels  10 us (18%)
  local copies, waits for them, and re-layouts  1.8 us (3%)
  between operations  0.91 us (2%)
    ppermute x16, starting transfers between devices, move(): return lax.ppermute(block, AXES, route)  29 us
    ppermute x16, waiting for transfers between devices, move(): return lax.ppermute(block, AXES, route)  13.3 us
    pallas_call x3, Pallas kernels, stage(): pl.pallas_call(kernel, out_shape=STATE + tuple(extra), in_specs=[SMEM] *...  5.19 us
    pallas_call x1, Pallas kernels, last_stage(): pl.pallas_call(last_kernel, out_shape=jax.ShapeDtypeStruct((TILES * TILE,...  2.2 us
    unnamed x12, local copies, waits for them, and re-layouts  1.8 us
    pallas_call x1, Pallas kernels, first_stage(): pl.pallas_call(first_kernel, out_shape=STATE + (jax.ShapeDtypeStruct((2 *...  1.35 us
  transfers between devices with their start and end apart: 16, of which 5 were waited for; matrix products, arithmetic and copies ran while one was open for 0% of the time, Pallas kernels for 14%

profile of v4, /device:TPU:1, one launch (start us, length us, event | category | flops | bytes accessed | tf_op | source)
XLA Modules:
  0.0 55.0 jit_solution(2527774019956459535)
XLA Ops:
  0.0 0.0 copy-start
  0.0 0.0 copy-start.1
  0.0 0.0 copy-start.2
  0.0 1.1 %copy-done.2 = bf16[512,512]{1,0:T(8,128)(2,1)S(1)} copy-done((bf16[512,512]{1,0:T(8,128)(2,1)S(1)}, bf16[512,512]{1,0:T(8,128)(2,1)}, u32[]{:S(2)}) %copy-start.2) | copy-done | bytes 524312
  1.1 0.0 copy-start.3
  1.1 0.0 copy-start.4
  1.1 0.4 split_keys.1
  1.5 3.1 %collective-permute-start.8 = (bf16[128,512]{1,0:T(8,128)(2,1)S(1)}, bf16[128,512]{1,0:T(8,128)(2,1)S(1)}, u32[]{:S(2)}, u32[]{:S(2)}) collective-permute-start(bf16[128,512]{1,0:T(8,128)(2,1)S(1)} %get-tuple-element.30), channel_id=1, source_target_pairs={{0,3},{1,2},{2,1},{3,0},{4,7},{5,6},{6,5},{7,4},{8,11},{9,10},{10,... | collective-permute-start | bytes 393224 | tf_op jit(solution)/shard_map/ppermute | solution.py:37
  4.6 0.1 collective-permute-start.9
  4.7 4.3 %collective-permute-done.8.b0 = bf16[128,512]{1,0:T(8,128)(2,1)S(1)} collective-permute-done((bf16[128,512]{1,0:T(8,128)(2,1)S(1)}, bf16[128,512]{1,0:T(8,128)(2,1)S(1)}, u32[]{:S(2)}, u32[]{:S(2)}) %collective-permute-start.8) | collective-permute-done | bytes 131104 | tf_op jit(solution)/shard_map/ppermute | solution.py:37
  9.0 3.6 %collective-permute-start.12 = (bf16[128,512]{1,0:T(8,128)(2,1)S(1)}, bf16[128,512]{1,0:T(8,128)(2,1)S(1)}, u32[]{:S(2)}, u32[]{:S(2)}) collective-permute-start(bf16[128,512]{1,0:T(8,128)(2,1)S(1)} %collective-permute-done.8.b0), channel_id=1, source_target_pairs={{0,67},{1,66},{2,65},{3,64},{4,71},{5,70},{6,69},{7,68},{8,75},{9,... | collective-permute-start | bytes 393224 | tf_op jit(solution)/shard_map/ppermute | solution.py:37
  12.5 0.0 copy-done
  12.5 0.0 copy-done.1
  12.5 0.0 copy-start.5
  12.5 0.7 %copy-done.5 = s32[1,4]{1,0:T(1,128)S(1)} copy-done((s32[1,4]{1,0:T(1,128)S(1)}, s32[1,4]{1,0:T(1,128)}, u32[]{:S(2)}) %copy-start.5) | copy-done | bytes 40
  13.2 0.9 %prepare.1 = (bf16[272,512]{1,0:T(8,128)(2,1)S(1)}, bf16[256,512]{1,0:T(8,128)(2,1)S(1)}, bf16[512,512]{1,0:T(8,128)(2,1)S(1)}, bf16[4,4,128,256]{3,2,1,0:T(8,128)(2,1)S(1)}) custom-call(bf16[512,512]{1,0:T(8,128)(2,1)S(1)} %copy-done, bf16[512,512]{1,0:T(8,128)(2,1)S(1)} %copy-done.1, s32[1,4]{1,0:T(1,128)S(1)} %copy-done.5), custom_call_target="tpu_custom_call" | custom-call | flops 40000000 | bytes 1048576 | tf_op jit(solution)/shard_map/prepare/pallas_call | solution.py:110
  14.1 0.1 collective-permute-start.3
  14.2 1.7 %collective-permute-start.1 = (bf16[256,512]{1,0:T(8,128)(2,1)S(1)}, bf16[256,512]{1,0:T(8,128)(2,1)S(1)}, u32[]{:S(2)}, u32[]{:S(2)}) collective-permute-start(bf16[256,512]{1,0:T(8,128)(2,1)S(1)} %get-tuple-element.26), channel_id=1, source_target_pairs={{0,3},{1,2},{2,1},{3,0},{4,7},{5,6},{6,5},{7,4},{8,11},{9,10},{10,... | collective-permute-start | bytes 786440 | tf_op jit(solution)/shard_map/ppermute | solution.py:37
  15.9 0.1 collective-permute-start.15
  16.1 0.0 collective-permute-done.9.b1
  16.1 0.0 copy-done.3
  16.1 0.4 collective-permute-start.14
  16.4 0.0 collective-permute-done.12.kc0
  16.4 2.8 %collective-permute-start.13 = (bf16[128,512]{1,0:T(8,128)(2,1)S(1)}, bf16[128,512]{1,0:T(8,128)(2,1)S(1)}, u32[]{:S(2)}, u32[]{:S(2)}) collective-permute-start(bf16[128,512]{1,0:T(8,128)(2,1)S(1)} %collective-permute-done.9.b1), channel_id=1, source_target_pairs={{0,67},{1,66},{2,65},{3,64},{4,71},{5,70},{6,69},{7,68},{8,75},{9,... | collective-permute-start | bytes 393224 | tf_op jit(solution)/shard_map/ppermute | solution.py:37
  19.2 3.7 %collective-permute-done.13.kc1 = bf16[128,512]{1,0:T(8,128)(2,1)S(1)} collective-permute-done((bf16[128,512]{1,0:T(8,128)(2,1)S(1)}, bf16[128,512]{1,0:T(8,128)(2,1)S(1)}, u32[]{:S(2)}, u32[]{:S(2)}) %collective-permute-start.13) | collective-permute-done | bytes 131104 | tf_op jit(solution)/shard_map/ppermute | solution.py:37
  22.9 3.0 %collective-permute-start.5 = (bf16[256,512]{1,0:T(8,128)(2,1)S(1)}, bf16[256,512]{1,0:T(8,128)(2,1)S(1)}, u32[]{:S(2)}, u32[]{:S(2)}) collective-permute-start(bf16[256,512]{1,0:T(8,128)(2,1)S(1)} %get-tuple-element.25), channel_id=1, source_target_pairs={{0,67},{1,66},{2,65},{3,64},{4,71},{5,70},{6,69},{7,68},{8,75},{9,... | collective-permute-start | bytes 786440 | tf_op jit(solution)/shard_map/ppermute | solution.py:37
  26.5 0.0 copy-done.4
  26.5 1.4 %first_stage.1 = (f32[5,512,128]{2,1,0:T(8,128)S(1)}, f32[5,8,128]{2,1,0:T(8,128)S(1)}, f32[5,8,128]{2,1,0:T(8,128)S(1)}, bf16[256,512]{1,0:T(8,128)(2,1)S(1)}) custom-call(s32[4,6]{1,0:T(4,128)S(1)} %copy-done.4, s32[1]{0:T(128)S(6)} %copy.25.live, bf16[512,512]{1,0:T(8,128)(2,1)S(1)} %copy-done.3, bf16[512,512]{1,0:T(8,128)(2,1)S(1)} %get-tuple-element.29.v_ref, ...), custom_call_target="tpu_custom_call" | custom-call | flops 320000000 | bytes 1048576 | tf_op jit(solution)/shard_map/first_stage/pallas_call | solution.py:209
  27.9 0.6 %collective-permute-done.1.vb = bf16[256,512]{1,0:T(8,128)(2,1)S(1)} collective-permute-done((bf16[256,512]{1,0:T(8,128)(2,1)S(1)}, bf16[256,512]{1,0:T(8,128)(2,1)S(1)}, u32[]{:S(2)}, u32[]{:S(2)}) %collective-permute-start.1) | collective-permute-done | bytes 262176 | tf_op jit(solution)/shard_map/ppermute | solution.py:37
  28.5 4.9 %collective-permute-start.10 = (bf16[256,512]{1,0:T(8,128)(2,1)S(1)}, bf16[256,512]{1,0:T(8,128)(2,1)S(1)}, u32[]{:S(2)}, u32[]{:S(2)}) collective-permute-start(bf16[256,512]{1,0:T(8,128)(2,1)S(1)} %get-tuple-element.32.kb), channel_id=1, source_target_pairs={{0,4},{1,61},{2,6},{3,63},{4,8},{5,1},{6,10},{7,3},{8,12},{9,5},{1... | collective-permute-start | bytes 786440 | tf_op jit(solution)/shard_map/ppermute | solution.py:37
  33.4 0.0 collective-permute-done.3.vb
  33.4 0.0 collective-permute-start.4
  33.4 0.0 collective-permute-done.5
  33.4 4.1 %collective-permute-start.11 = (bf16[272,512]{1,0:T(8,128)(2,1)S(1)}, bf16[272,512]{1,0:T(8,128)(2,1)S(1)}, u32[]{:S(2)}, u32[]{:S(2)}) collective-permute-start(bf16[272,512]{1,0:T(8,128)(2,1)S(1)} %collective-permute-done.3.vb), channel_id=1, source_target_pairs={{0,4},{1,61},{2,6},{3,63},{4,8},{5,1},{6,10},{7,3},{8,12},{9,5},{1... | collective-permute-start | bytes 835592 | tf_op jit(solution)/shard_map/ppermute | solution.py:37
  37.5 0.0 collective-permute-done.10.kd
  37.5 0.6 %collective-permute-start.7 = (bf16[256,512]{1,0:T(8,128)(2,1)S(1)}, bf16[256,512]{1,0:T(8,128)(2,1)S(1)}, u32[]{:S(2)}, u32[]{:S(2)}) collective-permute-start(bf16[256,512]{1,0:T(8,128)(2,1)S(1)} %collective-permute-done.1.vb), channel_id=1, source_target_pairs={{0,67},{1,66},{2,65},{3,64},{4,71},{5,70},{6,69},{7,68},{8,75},{9,... | collective-permute-start | bytes 786440 | tf_op jit(solution)/shard_map/ppermute | solution.py:37
  38.1 0.0 collective-permute-done.15.v_ref
  38.1 0.0 collective-permute-start.6
  38.1 0.0 collective-permute-done.14.k_ref
  38.1 1.7 %collective-permute-start = (bf16[256,512]{1,0:T(8,128)(2,1)S(1)}, bf16[256,512]{1,0:T(8,128)(2,1)S(1)}, u32[]{:S(2)}, u32[]{:S(2)}) collective-permute-start(bf16[256,512]{1,0:T(8,128)(2,1)S(1)} %get-tuple-element.25), channel_id=1, source_target_pairs={{0,63},{1,2},{2,1},{3,4},{4,3},{5,6},{6,5},{7,8},{8,7},{9,10},{10,... | collective-permute-start | bytes 786440 | tf_op jit(solution)/shard_map/ppermute | solution.py:37
  39.9 1.0 %collective-permute-done.4.vc.marks = bf16[272,512]{1,0:T(8,128)(2,1)S(1)} collective-permute-done((bf16[272,512]{1,0:T(8,128)(2,1)S(1)}, bf16[272,512]{1,0:T(8,128)(2,1)S(1)}, u32[]{:S(2)}, u32[]{:S(2)}) %collective-permute-start.4) | collective-permute-done | bytes 278560 | tf_op jit(solution)/shard_map/ppermute | solution.py:37
  40.9 2.8 %collective-permute-start.2 = (bf16[256,512]{1,0:T(8,128)(2,1)S(1)}, bf16[256,512]{1,0:T(8,128)(2,1)S(1)}, u32[]{:S(2)}, u32[]{:S(2)}) collective-permute-start(bf16[256,512]{1,0:T(8,128)(2,1)S(1)} %collective-permute-done.1.vb), channel_id=1, source_target_pairs={{0,4},{1,61},{2,6},{3,63},{4,8},{5,1},{6,10},{7,3},{8,12},{9,5},{1... | collective-permute-start | bytes 786440 | tf_op jit(solution)/shard_map/ppermute | solution.py:37
  43.7 1.6 %shard_map.64 = (f32[5,512,128]{2,1,0:T(8,128)S(1)}, f32[5,8,128]{2,1,0:T(8,128)S(1)}, f32[5,8,128]{2,1,0:T(8,128)S(1)}) custom-call(s32[4,6]{1,0:T(4,128)S(1)} %copy-done.4, s32[1]{0:T(128)S(6)} %copy.25.live, bf16[512,512]{1,0:T(8,128)(2,1)S(1)} %collective-permute-done.14.k_ref, ...), custom_call_target="tpu_custom_call", output_to_operand_aliasing={{0}: (5, {}), {1}: (6, {}), {2}: (7, {})} | custom-call | flops 320000000 | bytes 1048576 | tf_op jit(solution)/shard_map/pallas_call | solution.py:299
  45.3 0.0 collective-permute-done.11.vd
  45.3 2.1 %shard_map.65 = (f32[5,512,128]{2,1,0:T(8,128)S(1)}, f32[5,8,128]{2,1,0:T(8,128)S(1)}, f32[5,8,128]{2,1,0:T(8,128)S(1)}) custom-call(s32[4,6]{1,0:T(4,128)S(1)} %copy-done.4, s32[1]{0:T(128)S(6)} %copy.25.live, bf16[256,512]{1,0:T(8,128)(2,1)S(1)} %get-tuple-element.32.kb, ...), custom_call_target="tpu_custom_call", output_to_operand_aliasing={{0}: (10, {}), {1}: (11, {}), {2}: (12, {})} | custom-call | flops 320000000 | bytes 1048576 | tf_op jit(solution)/shard_map/pallas_call | solution.py:299
  47.4 0.0 collective-permute-done.7.vc
  47.5 0.0 collective-permute-done.6.kc
  47.5 1.5 %shard_map.66 = (f32[5,512,128]{2,1,0:T(8,128)S(1)}, f32[5,8,128]{2,1,0:T(8,128)S(1)}, f32[5,8,128]{2,1,0:T(8,128)S(1)}) custom-call(s32[4,6]{1,0:T(4,128)S(1)} %copy-done.4, s32[1]{0:T(128)S(6)} %copy.25.live, bf16[272,512]{1,0:T(8,128)(2,1)S(1)} %collective-permute-done.4.vc.marks, ...), custom_call_target="tpu_custom_call", output_to_operand_aliasing={{0}: (6, {}), {1}: (7, {}), {2}: (8, {})} | custom-call | flops 320000000 | bytes 1048576 | tf_op jit(solution)/shard_map/pallas_call | solution.py:299
  49.0 3.7 %collective-permute-done.kb.kd = bf16[256,512]{1,0:T(8,128)(2,1)S(1)} collective-permute-done((bf16[256,512]{1,0:T(8,128)(2,1)S(1)}, bf16[256,512]{1,0:T(8,128)(2,1)S(1)}, u32[]{:S(2)}, u32[]{:S(2)}) %collective-permute-start) | collective-permute-done | bytes 262176 | tf_op jit(solution)/shard_map/ppermute | solution.py:37
  52.6 0.0 collective-permute-done.2.vd
  52.7 2.2 %last_stage.1 = bf16[512,512]{1,0:T(8,128)(2,1)} custom-call(s32[4,6]{1,0:T(4,128)S(1)} %copy-done.4, s32[1]{0:T(128)S(6)} %copy.25.live, bf16[256,512]{1,0:T(8,128)(2,1)S(1)} %collective-permute-done.kb.kd, bf16[256,512]{1,0:T(8,128)(2,1)S(1)} %collective-permute-done.1.vb, bf16[256,512]{1,0:T(8,128)(2,1)S(1)} %collective-permute-done.kb.kd, ...), custom_call_target="tpu_custom_call" | custom-call | flops 320000000 | bytes 1048576 | tf_op jit(solution)/shard_map/last_stage/pallas_call | solution.py:335
Async XLA Ops:
  0.0 12.5 %copy-start = (bf16[512,512]{1,0:T(8,128)(2,1)S(1)}, bf16[512,512]{1,0:T(8,128)(2,1)}, u32[]{:S(2)}) copy-start(bf16[512,512]{1,0:T(8,128)(2,1)} %q_ref.1) | copy-start | bytes 1572868
  0.0 12.5 %copy-start.1 = (bf16[512,512]{1,0:T(8,128)(2,1)S(1)}, bf16[512,512]{1,0:T(8,128)(2,1)}, u32[]{:S(2)}) copy-start(bf16[512,512]{1,0:T(8,128)(2,1)} %v_ref.1) | copy-start | bytes 1572868
  0.0 1.1 %copy-start.2 = (bf16[512,512]{1,0:T(8,128)(2,1)S(1)}, bf16[512,512]{1,0:T(8,128)(2,1)}, u32[]{:S(2)}) copy-start(bf16[512,512]{1,0:T(8,128)(2,1)} %k_ref.1) | copy-start | bytes 1572868
  1.1 14.9 %copy-start.3 = (bf16[512,512]{1,0:T(8,128)(2,1)S(1)}, bf16[512,512]{1,0:T(8,128)(2,1)}, u32[]{:S(2)}) copy-start(bf16[512,512]{1,0:T(8,128)(2,1)} %k_ref.1) | copy-start | bytes 1572868
  1.1 25.4 %copy-start.4 = (s32[4,6]{1,0:T(4,128)S(1)}, s32[4,6]{1,0:T(4,128)}, u32[]{:S(2)}) copy-start(s32[4,6]{1,0:T(4,128)} %lists.9) | copy-start | bytes 292
  1.5 7.4 %collective-permute-start.8 = (bf16[128,512]{1,0:T(8,128)(2,1)S(1)}, bf16[128,512]{1,0:T(8,128)(2,1)S(1)}, u32[]{:S(2)}, u32[]{:S(2)}) collective-permute-start(bf16[128,512]{1,0:T(8,128)(2,1)S(1)} %get-tuple-element.30), channel_id=1, source_target_pairs={{0,3},{1,2},{2,1},{3,0},{4,7},{5,6},{6,5},{7,4},{8,11},{9,10},{10,... | collective-permute-start | bytes 393224 | tf_op jit(solution)/shard_map/ppermute | solution.py:37
  4.6 11.5 %collective-permute-start.9 = (bf16[128,512]{1,0:T(8,128)(2,1)S(1)}, bf16[128,512]{1,0:T(8,128)(2,1)S(1)}, u32[]{:S(2)}, u32[]{:S(2)}) collective-permute-start(bf16[128,512]{1,0:T(8,128)(2,1)S(1)} %get-tuple-element.31), channel_id=1, source_target_pairs={{0,3},{1,2},{2,1},{3,0},{4,7},{5,6},{6,5},{7,4},{8,11},{9,10},{10,... | collective-permute-start | bytes 393224 | tf_op jit(solution)/shard_map/ppermute | solution.py:37
  9.0 7.5 %collective-permute-start.12 = (bf16[128,512]{1,0:T(8,128)(2,1)S(1)}, bf16[128,512]{1,0:T(8,128)(2,1)S(1)}, u32[]{:S(2)}, u32[]{:S(2)}) collective-permute-start(bf16[128,512]{1,0:T(8,128)(2,1)S(1)} %collective-permute-done.8.b0), channel_id=1, source_target_pairs={{0,67},{1,66},{2,65},{3,64},{4,71},{5,70},{6,69},{7,68},{8,75},{9,... | collective-permute-start | bytes 393224 | tf_op jit(solution)/shard_map/ppermute | solution.py:37
  12.5 0.7 %copy-start.5 = (s32[1,4]{1,0:T(1,128)S(1)}, s32[1,4]{1,0:T(1,128)}, u32[]{:S(2)}) copy-start(s32[1,4]{1,0:T(1,128)} %ids.1) | copy-start | bytes 52
  14.1 19.3 %collective-permute-start.3 = (bf16[272,512]{1,0:T(8,128)(2,1)S(1)}, bf16[272,512]{1,0:T(8,128)(2,1)S(1)}, u32[]{:S(2)}, u32[]{:S(2)}) collective-permute-start(bf16[272,512]{1,0:T(8,128)(2,1)S(1)} %get-tuple-element.28), channel_id=1, source_target_pairs={{0,3},{1,2},{2,1},{3,0},{4,7},{5,6},{6,5},{7,4},{8,11},{9,10},{10,... | collective-permute-start | bytes 835592 | tf_op jit(solution)/shard_map/ppermute | solution.py:37
  14.2 14.3 %collective-permute-start.1 = (bf16[256,512]{1,0:T(8,128)(2,1)S(1)}, bf16[256,512]{1,0:T(8,128)(2,1)S(1)}, u32[]{:S(2)}, u32[]{:S(2)}) collective-permute-start(bf16[256,512]{1,0:T(8,128)(2,1)S(1)} %get-tuple-element.26), channel_id=1, source_target_pairs={{0,3},{1,2},{2,1},{3,0},{4,7},{5,6},{6,5},{7,4},{8,11},{9,10},{10,... | collective-permute-start | bytes 786440 | tf_op jit(solution)/shard_map/ppermute | solution.py:37
  15.9 22.2 %collective-permute-start.15 = (bf16[512,512]{1,0:T(8,128)(2,1)S(1)}, bf16[512,512]{1,0:T(8,128)(2,1)S(1)}, u32[]{:S(2)}, u32[]{:S(2)}) collective-permute-start(bf16[512,512]{1,0:T(8,128)(2,1)S(1)} %get-tuple-element.29.v_ref), channel_id=1, source_target_pairs={{0,1},{1,0},{2,3},{3,2},{4,5},{5,4},{6,7},{7,6},{8,9},{9,8},{10,11... | collective-permute-start | bytes 1572872 | tf_op jit(solution)/shard_map/ppermute | solution.py:37
  16.1 22.1 %collective-permute-start.14 = (bf16[512,512]{1,0:T(8,128)(2,1)S(1)}, bf16[512,512]{1,0:T(8,128)(2,1)S(1)}, u32[]{:S(2)}, u32[]{:S(2)}) collective-permute-start(bf16[512,512]{1,0:T(8,128)(2,1)S(1)} %copy-done.3), channel_id=1, source_target_pairs={{0,1},{1,0},{2,3},{3,2},{4,5},{5,4},{6,7},{7,6},{8,9},{9,8},{10,11... | collective-permute-start | bytes 1572872 | tf_op jit(solution)/shard_map/ppermute | solution.py:37
  16.4 6.5 %collective-permute-start.13 = (bf16[128,512]{1,0:T(8,128)(2,1)S(1)}, bf16[128,512]{1,0:T(8,128)(2,1)S(1)}, u32[]{:S(2)}, u32[]{:S(2)}) collective-permute-start(bf16[128,512]{1,0:T(8,128)(2,1)S(1)} %collective-permute-done.9.b1), channel_id=1, source_target_pairs={{0,67},{1,66},{2,65},{3,64},{4,71},{5,70},{6,69},{7,68},{8,75},{9,... | collective-permute-start | bytes 393224 | tf_op jit(solution)/shard_map/ppermute | solution.py:37
  22.9 10.5 %collective-permute-start.5 = (bf16[256,512]{1,0:T(8,128)(2,1)S(1)}, bf16[256,512]{1,0:T(8,128)(2,1)S(1)}, u32[]{:S(2)}, u32[]{:S(2)}) collective-permute-start(bf16[256,512]{1,0:T(8,128)(2,1)S(1)} %get-tuple-element.25), channel_id=1, source_target_pairs={{0,67},{1,66},{2,65},{3,64},{4,71},{5,70},{6,69},{7,68},{8,75},{9,... | collective-permute-start | bytes 786440 | tf_op jit(solution)/shard_map/ppermute | solution.py:37
  28.5 9.0 %collective-permute-start.10 = (bf16[256,512]{1,0:T(8,128)(2,1)S(1)}, bf16[256,512]{1,0:T(8,128)(2,1)S(1)}, u32[]{:S(2)}, u32[]{:S(2)}) collective-permute-start(bf16[256,512]{1,0:T(8,128)(2,1)S(1)} %get-tuple-element.32.kb), channel_id=1, source_target_pairs={{0,4},{1,61},{2,6},{3,63},{4,8},{5,1},{6,10},{7,3},{8,12},{9,5},{1... | collective-permute-start | bytes 786440 | tf_op jit(solution)/shard_map/ppermute | solution.py:37
  33.4 7.5 %collective-permute-start.4 = (bf16[272,512]{1,0:T(8,128)(2,1)S(1)}, bf16[272,512]{1,0:T(8,128)(2,1)S(1)}, u32[]{:S(2)}, u32[]{:S(2)}) collective-permute-start(bf16[272,512]{1,0:T(8,128)(2,1)S(1)} %collective-permute-done.3.vb), channel_id=1, source_target_pairs={{0,67},{1,66},{2,65},{3,64},{4,71},{5,70},{6,69},{7,68},{8,75},{9,... | collective-permute-start | bytes 835592 | tf_op jit(solution)/shard_map/ppermute | solution.py:37
  33.4 11.9 %collective-permute-start.11 = (bf16[272,512]{1,0:T(8,128)(2,1)S(1)}, bf16[272,512]{1,0:T(8,128)(2,1)S(1)}, u32[]{:S(2)}, u32[]{:S(2)}) collective-permute-start(bf16[272,512]{1,0:T(8,128)(2,1)S(1)} %collective-permute-done.3.vb), channel_id=1, source_target_pairs={{0,4},{1,61},{2,6},{3,63},{4,8},{5,1},{6,10},{7,3},{8,12},{9,5},{1... | collective-permute-start | bytes 835592 | tf_op jit(solution)/shard_map/ppermute | solution.py:37
  37.5 9.9 %collective-permute-start.7 = (bf16[256,512]{1,0:T(8,128)(2,1)S(1)}, bf16[256,512]{1,0:T(8,128)(2,1)S(1)}, u32[]{:S(2)}, u32[]{:S(2)}) collective-permute-start(bf16[256,512]{1,0:T(8,128)(2,1)S(1)} %collective-permute-done.1.vb), channel_id=1, source_target_pairs={{0,67},{1,66},{2,65},{3,64},{4,71},{5,70},{6,69},{7,68},{8,75},{9,... | collective-permute-start | bytes 786440 | tf_op jit(solution)/shard_map/ppermute | solution.py:37
  38.1 9.3 %collective-permute-start.6 = (bf16[256,512]{1,0:T(8,128)(2,1)S(1)}, bf16[256,512]{1,0:T(8,128)(2,1)S(1)}, u32[]{:S(2)}, u32[]{:S(2)}) collective-permute-start(bf16[256,512]{1,0:T(8,128)(2,1)S(1)} %collective-permute-done.5), channel_id=1, source_target_pairs={{0,3},{1,2},{2,1},{3,0},{4,7},{5,6},{6,5},{7,4},{8,11},{9,10},{10,... | collective-permute-start | bytes 786440 | tf_op jit(solution)/shard_map/ppermute | solution.py:37
  38.1 14.5 %collective-permute-start = (bf16[256,512]{1,0:T(8,128)(2,1)S(1)}, bf16[256,512]{1,0:T(8,128)(2,1)S(1)}, u32[]{:S(2)}, u32[]{:S(2)}) collective-permute-start(bf16[256,512]{1,0:T(8,128)(2,1)S(1)} %get-tuple-element.25), channel_id=1, source_target_pairs={{0,63},{1,2},{2,1},{3,4},{4,3},{5,6},{6,5},{7,8},{8,7},{9,10},{10,... | collective-permute-start | bytes 786440 | tf_op jit(solution)/shard_map/ppermute | solution.py:37
  40.9 11.7 %collective-permute-start.2 = (bf16[256,512]{1,0:T(8,128)(2,1)S(1)}, bf16[256,512]{1,0:T(8,128)(2,1)S(1)}, u32[]{:S(2)}, u32[]{:S(2)}) collective-permute-start(bf16[256,512]{1,0:T(8,128)(2,1)S(1)} %collective-permute-done.1.vb), channel_id=1, source_target_pairs={{0,4},{1,61},{2,6},{3,63},{4,8},{5,1},{6,10},{7,3},{8,12},{9,5},{1... | collective-permute-start | bytes 786440 | tf_op jit(solution)/shard_map/ppermute | solution.py:37
